TPU v7x, 256 devices: a 2x2x32 block of a 4x8x32 slice. The times are simulated.
256 devices in a mesh: groups: 4 (over y, x), az: 64 (over z, core).
Axes of the slice: x: 2, y: 2, z: 32, core: 2. Of those that a mesh axis runs over, the one named last changes fastest.
The devices are a block of a 4x8x32 slice.
Arguments:
- sweep_stack: bfloat16 [2, 4, 256, 80, 2560], P(None, None, ('groups', 'az')), parts along dimension 2
- blend_curve: bfloat16 [256, 80], P(('groups', 'az')), parts along dimension 0, may hold values from 0.25 to 4
- sweep_start_index: int32 [256], P(('groups', 'az')), parts along dimension 0, may hold values from -20 to 2530, as said below
- usable_azimuth_extent: int32 [256, 2], P(('groups', 'az')), parts along dimension 0, may hold values from 0 to 80, as said below
- usable_column_extent: int32 [256, 2], P(('groups', 'az')), parts along dimension 0, may hold values from 0 to 2560, as said below
- image_couples: int32 [16, 2], P('groups'), parts along dimension 0, may hold values from 0 to 3, as said below
Outputs:
- interferogram: float32 [2, 16, 512, 128], P(None, 'groups', 'az'), parts along dimension 1
- coherence: float32 [16, 512, 128], P('groups', 'az'), parts along dimension 0
There are 4 independent parts, one for each index of `groups`. A program takes and returns all parts, laid end to end along the dimension named above; each array names one. Nothing has to cross between parts.
Inputs may be any that keep to these rules, and one draw needn't show every extreme that they name: `sweep_start_index`: the valid lines of burst b lie at merged rows from b * 40 - 15 to (b + 1) * 40 + 14, and some burst reaches both ends. The valid lines of all bursts together cover every merged row from 0 to 2559. `usable_azimuth_extent`: first below end for every burst. `usable_column_extent`: first below end for every burst. `image_couples`: the two acquisitions of a pair differ.
All inputs are finite; a program needn't handle non-finite values.
Results may differ from a plain program's by a relative error of at most 0.0003.
Values may be sent and summed in bfloat16 or wider, within the bound.
No kernel may reach another device: no remote copies, remote signals or barrier semaphores. Data moves between devices by JAX's collectives and lax.ppermute only.
A program may use at most 64 MiB of HBM per device.

v0:
```python
import jax
import jax.numpy as jnp
from jax import lax
from jax.sharding import PartitionSpec as P

BLOCK_HEIGHT = 40
SLANT_WIDTH = 2560
LOOK_ROWS = 5
LOOK_COLS = 20
MARGIN = 15
SWEEP_HEIGHT = 80


def from_behind(block, axis, distance):
    devices = range(lax.axis_size(axis))
    route = [(i - distance, i) for i in devices if i - distance in devices]
    return lax.ppermute(block, axis, route)


def looked(values, column_box):
    shaped = values.reshape(
        values.shape[:-2] + (values.shape[-2] // LOOK_ROWS, LOOK_ROWS, values.shape[-1])
    )
    aggregate = jnp.sum(shaped, axis=-2)
    return jnp.dot(aggregate, column_box, precision=lax.Precision.HIGHEST)


def weighted(raw_lines, weights):
    return raw_lines.astype(jnp.float32) * weights.astype(jnp.float32)[:, None]


def per_device(
    sweep_stack,
    blend_curve,
    sweep_start_index,
    usable_azimuth_extent,
    usable_column_extent,
    image_couples,
):
    sweep_content = sweep_stack[:, :, 0]
    block_height = BLOCK_HEIGHT
    azimuth_index = jnp.arange(SWEEP_HEIGHT, dtype=jnp.int32)
    column_index = jnp.arange(SLANT_WIDTH, dtype=jnp.int32)
    line_valid = (azimuth_index >= usable_azimuth_extent[0, 0]) & (
        azimuth_index < usable_azimuth_extent[0, 1]
    )
    azimuth_blend = jnp.where(line_valid, blend_curve[0], jnp.zeros((), jnp.bfloat16))
    sample_valid = (column_index >= usable_column_extent[0, 0]) & (
        column_index < usable_column_extent[0, 1]
    )
    index_shift = sweep_start_index[0] - (lax.axis_index("az") - 1) * block_height

    def gather_lines(start_index, count):
        desired = start_index + jnp.arange(count, dtype=jnp.int32) - index_shift
        within_extent = (desired >= 0) & (desired < SWEEP_HEIGHT)
        bounded_indices = jnp.clip(desired, 0, SWEEP_HEIGHT - 1)
        chosen_indices = jnp.take(sweep_content, bounded_indices, axis=2)
        raw_lines = jnp.where(sample_valid, chosen_indices, jnp.zeros((), jnp.bfloat16))
        matches = bounded_indices[:, None] == azimuth_index[None, :]
        weights = jnp.sum(
            jnp.where(matches, azimuth_blend[None, :], jnp.zeros((), jnp.bfloat16)), axis=1
        )
        weights = jnp.where(within_extent, weights, jnp.zeros((), jnp.bfloat16))
        return (raw_lines, weights)

    extent_rows = MARGIN
    middle_lines, middle_weights = gather_lines(block_height, block_height)
    lower_lines, lower_weights = gather_lines(block_height - extent_rows, extent_rows)
    upper_lines, upper_weights = gather_lines(2 * block_height, extent_rows)
    above_lines, above_weights = from_behind((lower_lines, lower_weights), "az", -1)
    below_lines, below_weights = from_behind((upper_lines, upper_weights), "az", 1)
    from_above = weighted(above_lines, above_weights)
    from_below = weighted(below_lines, below_weights)
    cross_term = weighted(middle_lines, middle_weights)
    cross_term = cross_term.at[:, :, block_height - extent_rows :].add(from_above)
    cross_term = cross_term.at[:, :, :extent_rows].add(from_below)
    intensity_norm = middle_weights.astype(jnp.float32)
    intensity_norm = intensity_norm.at[block_height - extent_rows :].add(
        above_weights.astype(jnp.float32)
    )
    intensity_norm = intensity_norm.at[:extent_rows].add(below_weights.astype(jnp.float32))
    combined_grid = cross_term / intensity_norm[:, None]
    intensity = combined_grid[0] * combined_grid[0] + combined_grid[1] * combined_grid[1]
    first_image = jnp.take(combined_grid, image_couples[:, 0], axis=1)
    second_image = jnp.take(combined_grid, image_couples[:, 1], axis=1)
    real_part = first_image[0] * second_image[0] + first_image[1] * second_image[1]
    imag_part = first_image[1] * second_image[0] - first_image[0] * second_image[1]
    column_box = (
        column_index[:, None] // LOOK_COLS
        == jnp.arange(SLANT_WIDTH // LOOK_COLS, dtype=jnp.int32)[None, :]
    ).astype(jnp.float32)
    look_sum = looked(jnp.stack([real_part, imag_part]), column_box)
    look_power = looked(intensity, column_box)
    power_first = jnp.take(look_power, image_couples[:, 0], axis=0)
    power_second = jnp.take(look_power, image_couples[:, 1], axis=0)
    coherence = (look_sum[0] * look_sum[0] + look_sum[1] * look_sum[1]) / jnp.maximum(
        power_first * power_second, 1.0
    )
    interferogram = look_sum / (LOOK_ROWS * LOOK_COLS)
    return (interferogram, coherence)


def solution(mesh):
    return jax.shard_map(
        per_device,
        mesh=mesh,
        in_specs=(
            P(None, None, ("groups", "az"), None, None),
            P(("groups", "az"), None),
            P(("groups", "az")),
            P(("groups", "az"), None),
            P(("groups", "az"), None),
            P("groups", None),
        ),
        out_specs=(P(None, "groups", "az", None), P("groups", "az", None)),
        check_vma=False,
    )
```

profile of v0, /device:TPU:37, one launch (start us, length us, event | category | flops | bytes accessed | tf_op | source)
XLA Modules:
  0.0 83.8 jit_solution(6345981178381013266)
XLA Ops:
  1.3 1.4 %fusion.33 = (s32[1,1]{1,0:T(1,128)}, s32[1,1]{1,0:T(1,128)}) fusion(s32[1,2]{1,0:T(1,128)} %param.23), kind=kLoop, calls=%fused_computation.92 | loop fusion | bytes 16 | tf_op jit(solution)/shard_map/slice | solution.py:44
  2.7 1.9 %fusion.27 = bf16[80]{0:T(256)(128)(2,1)S(1)} fusion(bf16[1,80]{1,0:T(2,128)(2,1)} %param.21, s32[]{:T(128)} %bitcast.7, s32[]{:T(128)} %bitcast.6), kind=kLoop, calls=%fused_computation.85 | loop fusion | flops 320 | bytes 328 | tf_op jit(solution)/shard_map/jit(_where)/broadcast_in_dim | solution.py:61
  4.6 0.2 fusion.24
  4.8 22.4 %collective-permute-start.1 = (bf16[15]{0:T(256)(128)(2,1)S(1)}, bf16[15]{0:T(256)(128)(2,1)S(1)}, u32[]{:S(2)}, u32[]{:S(2)}) collective-permute-start(bf16[15]{0:T(256)(128)(2,1)S(1)} %and_select_fusion.1), channel_id=1, source_target_pairs={{1,0},{2,1},{3,2},{4,3},{5,4},{6,5},{7,6},{8,7},{9,8},{10,9},{11,1... | collective-permute-start | bytes 98 | tf_op jit(solution)/shard_map/ppermute | solution.py:17
  27.2 2.0 %collective-permute-start.3 = (bf16[15]{0:T(256)(128)(2,1)S(1)}, bf16[15]{0:T(256)(128)(2,1)S(1)}, u32[]{:S(2)}, u32[]{:S(2)}) collective-permute-start(bf16[15]{0:T(256)(128)(2,1)S(1)} %and_select_fusion), channel_id=1, source_target_pairs={{0,1},{1,2},{2,3},{3,4},{4,5},{5,6},{6,7},{7,8},{8,9},{9,10},{10,1... | collective-permute-start | bytes 98 | tf_op jit(solution)/shard_map/ppermute | solution.py:17
  29.2 1.3 %fusion.32 = (s32[1,1]{1,0:T(1,128)}, s32[1,1]{1,0:T(1,128)}) fusion(s32[1,2]{1,0:T(1,128)} %param.24), kind=kLoop, calls=%fused_computation.91 | loop fusion | bytes 16 | tf_op jit(solution)/shard_map/slice | solution.py:48
  30.5 4.5 %copy.51 = bf16[2,4,1,80,2560]{4,1,3,0,2:T(4,128)(2,1)S(1)} copy(bf16[2,4,1,80,2560]{4,3,2,1,0:T(8,128)(2,1)} %param.20) | data formatting | bytes 6553600 | tf_op args[0]
  35.0 1.9 %gather_fusion.2 = bf16[15,2,4,2560]{3,2,1,0:T(4,128)(2,1)} fusion(bf16[2,4,80,2560]{3,1,2,0:T(4,128)(2,1)S(1)} %bitcast.48, s32[1024]{0:T(1024)S(1)} %pad_clamp_fusion.2), kind=kCustom, calls=%fused_computation.3.clone | custom fusion | bytes 1228860 | tf_op jit(solution)/shard_map/jit(_take)/gather | solution.py:57
  36.8 0.0 copy-start.1
  36.8 1.9 %gather_fusion.1 = bf16[15,2,4,2560]{3,2,1,0:T(4,128)(2,1)} fusion(bf16[2,4,80,2560]{3,1,2,0:T(4,128)(2,1)S(1)} %bitcast.49, s32[1024]{0:T(1024)S(1)} %pad_clamp_fusion.3), kind=kCustom, calls=%fused_computation.clone | custom fusion | bytes 1228860 | tf_op jit(solution)/shard_map/jit(_take)/gather | solution.py:57
  38.7 1.3 %fusion.19 = pred[2560]{0:T(1024)(128)(4,1)S(1)} fusion(s32[]{:T(128)} %bitcast.2, s32[]{:T(128)} %bitcast.1), kind=kLoop, calls=%fused_computation.51 | loop fusion | flops 7680 | bytes 2568 | tf_op jit(solution)/shard_map/and | solution.py:48
  40.0 3.0 %bitcast_select_fusion = (bf16[2,4,15,2560]{3,1,0,2:T(4,128)(2,1)}, bf16[2,4,15,2560]{3,1,0,2:T(4,128)(2,1)}) fusion(bf16[15,2,4,2560]{3,2,1,0:T(4,128)(2,1)} %gather_fusion.2, pred[15]{0:T(512)(128)(4,1)S(1)} %get-tuple-element.77, pred[2560]{0:T(1024)(128)(4,1)S(1)} %fusion.19, bf16[15,2,4,2560]{3,2,1,0:T(4,128)(2,1)} %gather_fusion.1, ...), kind=kLoop, calls=%fused_computation.29 | loop fusion | flops 1228800 | bytes 2460190 | tf_op jit(solution)/shard_map/jit(_where)/select_n | solution.py:58
  43.0 1.9 %collective-permute-start.2 = (bf16[2,4,15,2560]{3,1,0,2:T(4,128)(2,1)}, bf16[2,4,15,2560]{3,1,0,2:T(4,128)(2,1)}, u32[]{:S(2)}, u32[]{:S(2)}) collective-permute-start(bf16[2,4,15,2560]{3,1,0,2:T(4,128)(2,1)} %get-tuple-element.65), channel_id=1, source_target_pairs={{0,1},{1,2},{2,3},{3,4},{4,5},{5,6},{6,7},{7,8},{8,9},{9,10},{10,1... | collective-permute-start | bytes 1843208 | tf_op jit(solution)/shard_map/ppermute | solution.py:17
  45.0 3.4 %collective-permute-start = (bf16[2,4,15,2560]{3,1,0,2:T(4,128)(2,1)}, bf16[2,4,15,2560]{3,1,0,2:T(4,128)(2,1)}, u32[]{:S(2)}, u32[]{:S(2)}) collective-permute-start(bf16[2,4,15,2560]{3,1,0,2:T(4,128)(2,1)} %get-tuple-element.66), channel_id=1, source_target_pairs={{1,0},{2,1},{3,2},{4,3},{5,4},{6,5},{7,6},{8,7},{9,8},{10,9},{11,1... | collective-permute-start | bytes 1843208 | tf_op jit(solution)/shard_map/ppermute | solution.py:17
  48.4 0.2 fusion.21
  48.6 0.0 copy-done.1
  48.7 3.4 %gather_fusion = bf16[40,2,4,2560]{3,2,1,0:T(4,128)(2,1)} fusion(bf16[2,4,80,2560]{3,1,2,0:T(4,128)(2,1)S(1)} %bitcast.50, s32[1024]{0:T(1024)S(1)} %pad_clamp_fusion.4), kind=kCustom, calls=%fused_computation.6 | custom fusion | bytes 3276960 | tf_op jit(solution)/shard_map/jit(_take)/gather | solution.py:57
  52.1 2.6 %multiply_bitcast_fusion = f32[2,4,40,2560]{3,1,0,2:T(4,128)S(1)} fusion(f32[40]{0:T(128)S(1)} %fusion.28, bf16[40,2,4,2560]{3,2,1,0:T(4,128)(2,1)} %gather_fusion, pred[40]{0:T(512)(128)(4,1)S(1)} %compare_and_fusion.4, pred[2560]{0:T(1024)(128)(4,1)S(1)} %fusion.19), kind=kLoop, calls=%fused_computation.11 | loop fusion | flops 3276800 | bytes 4917960 | tf_op jit(solution)/shard_map/mul | solution.py:29
  54.7 0.0 collective-permute-done.1
  54.7 0.0 collective-permute-done.3
  54.7 0.1 add_dynamic-update-slice_fusion
  54.9 1.9 %collective-permute-done = bf16[2,4,15,2560]{3,1,0,2:T(4,128)(2,1)} collective-permute-done((bf16[2,4,15,2560]{3,1,0,2:T(4,128)(2,1)}, bf16[2,4,15,2560]{3,1,0,2:T(4,128)(2,1)}, u32[]{:S(2)}, u32[]{:S(2)}) %collective-permute-start) | collective-permute-done | bytes 614432 | tf_op jit(solution)/shard_map/ppermute | solution.py:17
  56.8 1.6 %fusion.8 = f32[2,4,40,2560]{3,1,0,2:T(4,128)S(1)} fusion(f32[2,4,40,2560]{3,1,0,2:T(4,128)S(1)} %multiply_bitcast_fusion, bf16[2,4,15,2560]{3,1,0,2:T(4,128)(2,1)} %collective-permute-done, f32[15]{0:T(128)S(1)} %convert_element_type.35), kind=kLoop, calls=%fused_computation.26 | loop fusion | flops 921600 | bytes 3072512 | tf_op jit(solution)/shard_map/scatter-add | solution.py:75
  58.4 0.0 collective-permute-done.2
  58.4 1.6 %fusion.7 = f32[2,4,40,2560]{3,1,0,2:T(4,128)S(1)} fusion(f32[2,4,40,2560]{3,1,0,2:T(4,128)S(1)} %fusion.8, bf16[2,4,15,2560]{3,1,0,2:T(4,128)(2,1)} %collective-permute-done.2, f32[15]{0:T(128)S(1)} %convert_element_type.37), kind=kLoop, calls=%fused_computation.24 | loop fusion | flops 921600 | bytes 3072512 | tf_op jit(solution)/shard_map/scatter-add | solution.py:76
  60.1 0.9 %broadcast_divide_fusion = f32[2,4,40,2560]{3,1,0,2:T(4,128)S(1)} fusion(f32[2,4,40,2560]{3,1,0,2:T(4,128)S(1)} %fusion.7, f32[40]{0:T(128)S(1)} %constant_dynamic-update-slice_fusion), kind=kLoop, calls=%fused_computation.17 | loop fusion | flops 819200 | bytes 6553760 | tf_op jit(solution)/shard_map/div | solution.py:82
  61.0 1.6 %fusion = f32[1,4,40,2560]{3,1,0,2:T(4,128)} fusion(f32[2,4,40,2560]{3,1,0,2:T(4,128)S(1)} %broadcast_divide_fusion), kind=kLoop, calls=%fused_computation.13 | loop fusion | flops 1228800 | bytes 4915200 | tf_op jit(solution)/shard_map/add | solution.py:83
  62.6 1.9 %copy.29 = f32[2,4,40,2560]{3,2,1,0:T(8,128)S(1)} copy(f32[2,4,40,2560]{3,1,0,2:T(4,128)S(1)} %broadcast_divide_fusion) | data formatting | bytes 6553600 | tf_op jit(solution)/shard_map/div | solution.py:82
  64.5 2.5 %reduce_sum.58 = f32[4,8,2560]{2,0,1:T(4,128)} reduce(f32[4,8,5,2560]{3,0,2,1:T(4,128)} %bitcast.52, f32[]{:T(128)} %constant.178.clone.1), dimensions={2}, to_apply=%region_4.7 | reduce | flops 327680 | bytes 1966084 | tf_op jit(solution)/shard_map/reduce_sum | solution.py:24
  67.0 1.8 %fusion.5 = f32[4,8,128]{2,0,1:T(4,128)S(1)} fusion(f32[4,8,2560]{2,0,1:T(4,128)} %reduce_sum.58, s32[2560]{0:T(1024)S(1)} %add_select_fusion), kind=kOutput, calls=%fused_computation.22 | convolution fusion | flops 126156800 | bytes 354304 | tf_op jit(solution)/shard_map/dot_general | solution.py:25
  68.8 0.6 gather_fusion.6
  69.3 0.6 gather_fusion.5
  69.9 2.4 %gather_fusion.3 = f32[4,2,40,2560]{3,2,1,0:T(8,128)} fusion(f32[2,4,40,2560]{3,2,1,0:T(8,128)S(1)} %copy.29, s32[1024]{0:T(1024)S(1)} %get-tuple-element.82), kind=kCustom, calls=%fused_computation.1.clone | custom fusion | bytes 6553616 | tf_op jit(solution)/shard_map/jit(_take)/gather | solution.py:84
  72.3 2.5 %gather_fusion.4 = f32[4,2,40,2560]{3,2,1,0:T(8,128)} fusion(f32[2,4,40,2560]{3,2,1,0:T(8,128)S(1)} %copy.29, s32[1024]{0:T(1024)S(1)} %get-tuple-element.81), kind=kCustom, calls=%fused_computation.4.clone | custom fusion | bytes 6553616 | tf_op jit(solution)/shard_map/jit(_take)/gather | solution.py:85
  74.8 0.0 copy-start
  74.8 2.5 %select_bitcast_fusion = f32[2,4,40,2560]{3,2,0,1:T(8,128)S(1)} fusion(f32[4,2,40,2560]{3,2,1,0:T(8,128)} %gather_fusion.4, pred[4]{0:T(512)(128)(4,1)S(1)} %get-tuple-element.67), kind=kLoop, calls=%fused_computation.9 | loop fusion | flops 819200 | bytes 6553604 | tf_op jit(solution)/shard_map/jit(_take)/select_n | solution.py:85
  77.3 0.4 copy-done
  77.7 0.4 select_bitcast_fusion.1
  78.1 0.6 multiply_add_fusion
  78.7 1.1 %copy.31 = f32[1,4,40,2560]{3,1,2,0:T(4,128)S(1)} copy(f32[1,4,40,2560]{3,2,0,1:T(8,128)S(1)} %get-tuple-element.63) | data formatting | bytes 3276800 | tf_op jit(solution)/shard_map/add | solution.py:86
  79.7 1.1 %copy.32 = f32[1,4,40,2560]{3,1,2,0:T(4,128)S(1)} copy(f32[1,4,40,2560]{3,2,0,1:T(8,128)S(1)} %get-tuple-element.64) | data formatting | bytes 3276800 | tf_op jit(solution)/shard_map/sub | solution.py:87
  80.8 0.8 maximum_reduce_fusion
  81.6 0.9 %broadcast_multiply_fusion = (f32[2,4,8,128]{3,1,2,0:T(4,128)S(1)}, f32[2,4,8,128]{3,1,2,0:T(4,128)S(1)}) fusion(f32[2,4,8,2560]{3,1,2,0:T(4,128)S(1)} %maximum_reduce_fusion, s32[2560]{0:T(1024)S(1)} %add_select_fusion), kind=kOutput, calls=%fused_computation.46 | convolution fusion | flops 251994112 | bytes 731136 | tf_op jit(solution)/shard_map/dot_general | solution.py:25
  82.5 0.6 copy.37
  83.1 0.1 fusion.14
  83.2 0.6 copy.38
  (19 shorter events, 0.2 us)
Async XLA Ops:
  4.8 49.9 %collective-permute-start.1 = (bf16[15]{0:T(256)(128)(2,1)S(1)}, bf16[15]{0:T(256)(128)(2,1)S(1)}, u32[]{:S(2)}, u32[]{:S(2)}) collective-permute-start(bf16[15]{0:T(256)(128)(2,1)S(1)} %and_select_fusion.1), channel_id=1, source_target_pairs={{1,0},{2,1},{3,2},{4,3},{5,4},{6,5},{7,6},{8,7},{9,8},{10,9},{11,1... | collective-permute-start | bytes 98 | tf_op jit(solution)/shard_map/ppermute | solution.py:17
  27.2 27.6 %collective-permute-start.3 = (bf16[15]{0:T(256)(128)(2,1)S(1)}, bf16[15]{0:T(256)(128)(2,1)S(1)}, u32[]{:S(2)}, u32[]{:S(2)}) collective-permute-start(bf16[15]{0:T(256)(128)(2,1)S(1)} %and_select_fusion), channel_id=1, source_target_pairs={{0,1},{1,2},{2,3},{3,4},{4,5},{5,6},{6,7},{7,8},{8,9},{9,10},{10,1... | collective-permute-start | bytes 98 | tf_op jit(solution)/shard_map/ppermute | solution.py:17
  36.8 11.8 %copy-start.1 = (s32[4,2]{0,1:T(2,128)S(1)}, s32[4,2]{0,1:T(2,128)}, u32[]{:S(2)}) copy-start(s32[4,2]{0,1:T(2,128)} %param.25) | copy-start | bytes 100
  43.0 15.4 %collective-permute-start.2 = (bf16[2,4,15,2560]{3,1,0,2:T(4,128)(2,1)}, bf16[2,4,15,2560]{3,1,0,2:T(4,128)(2,1)}, u32[]{:S(2)}, u32[]{:S(2)}) collective-permute-start(bf16[2,4,15,2560]{3,1,0,2:T(4,128)(2,1)} %get-tuple-element.65), channel_id=1, source_target_pairs={{0,1},{1,2},{2,3},{3,4},{4,5},{5,6},{6,7},{7,8},{8,9},{9,10},{10,1... | collective-permute-start | bytes 1843208 | tf_op jit(solution)/shard_map/ppermute | solution.py:17
  45.0 11.8 %collective-permute-start = (bf16[2,4,15,2560]{3,1,0,2:T(4,128)(2,1)}, bf16[2,4,15,2560]{3,1,0,2:T(4,128)(2,1)}, u32[]{:S(2)}, u32[]{:S(2)}) collective-permute-start(bf16[2,4,15,2560]{3,1,0,2:T(4,128)(2,1)} %get-tuple-element.66), channel_id=1, source_target_pairs={{1,0},{2,1},{3,2},{4,3},{5,4},{6,5},{7,6},{8,7},{9,8},{10,9},{11,1... | collective-permute-start | bytes 1843208 | tf_op jit(solution)/shard_map/ppermute | solution.py:17
  74.8 2.9 %copy-start = (f32[4,2,40,2560]{3,2,1,0:T(8,128)S(1)}, f32[4,2,40,2560]{3,2,1,0:T(8,128)}, u32[]{:S(2)}) copy-start(f32[4,2,40,2560]{3,2,1,0:T(8,128)} %gather_fusion.3) | copy-start | bytes 9830404
where the time goes:
time: 84.3 us; the launch traced here: 83.8 us
  starting transfers between devices  29.7 us (35%)
  local copies, waits for them, and re-layouts  25.9 us (31%)
  other arithmetic  22.1 us (26%)
  matrix products  2.61 us (3%)
  waiting for transfers between devices  1.88 us (2%)
  between operations  1.55 us (2%)
    ppermute x4, starting transfers between devices, from_behind(): return lax.ppermute(block, axis, route)  29.7 us
    gather x3, local copies, waits for them, and re-layouts, gather_lines(): chosen_indices = jnp.take(sweep_content, bounded_indices, axis=2)  7.13 us
    unnamed x7, local copies, waits for them, and re-layouts  6.1 us
    reduce_sum x2, other arithmetic, looked(): aggregate = jnp.sum(shaped, axis=-2)  3.3 us
    select_n x1, other arithmetic, gather_lines(): jnp.where(sample_valid, chosen_indices, jnp.zeros((), jnp.bfloat16))  3.01 us
    mul x1, other arithmetic, weighted(): return raw_lines.astype(jnp.float32) * weights.astype(jnp.float32)[:, None]  2.61 us
    dot_general x2, matrix products, looked(): return jnp.dot(aggregate, column_box, precision=lax.Precision.HIGHEST)  2.61 us
    select_n x1, other arithmetic, per_device(): second_image = jnp.take(combined_grid, image_couples[:, 1], axis=1)  2.49 us
  transfers between devices with their start and end apart: 4, of which 1 were waited for; matrix products, arithmetic and copies ran while one was open for 26% of the time, Pallas kernels for 0%

commit v1 on v0

v1 whole, which is shorter than its diff:
```python
import jax
import jax.numpy as jnp
from jax import lax
from jax.experimental import pallas as pl
from jax.experimental.pallas import tpu as pltpu
from jax.sharding import PartitionSpec as P

BLOCK_HEIGHT = 40
SLANT_WIDTH = 2560
LOOK_ROWS = 5
LOOK_COLS = 20
MARGIN = 15
SWEEP_HEIGHT = 80
IMAGES = 4
PLANES = 2 * IMAGES
PAIRS = 4
SENT = 16
WINDOW = 32
LOOKS = SLANT_WIDTH // LOOK_COLS
BOXES = BLOCK_HEIGHT // LOOK_ROWS
TILE = 256
TILES = SLANT_WIDTH // TILE
F32 = jnp.float32
BF16 = jnp.bfloat16

HBM = pl.BlockSpec(memory_space=pltpu.HBM)
VMEM = pl.BlockSpec(memory_space=pltpu.VMEM)
SMEM = pl.BlockSpec(memory_space=pltpu.SMEM)


def iota(shape, dim):
    return lax.broadcasted_iota(jnp.int32, shape, dim)


def line_offset(start_ref):
    return lax.axis_index("az") * BLOCK_HEIGHT - start_ref[0]


def pack_kernel(start_ref, lines_ref, cols_ref, curve_ref, x_ref, a_ref, b_ref, win, sems):
    az = lax.axis_index("az")
    odd = lax.rem(az, 2)
    offset = line_offset(start_ref)
    down = offset - MARGIN
    up = offset + BLOCK_HEIGHT
    firsts = (jnp.where(odd == 1, down, up), jnp.where(odd == 1, up, down))
    copies = []
    bases = []
    for side in range(2):
        base = jnp.clip(
            lax.shift_left(lax.shift_right_arithmetic(firsts[side], 4), 4),
            0,
            SWEEP_HEIGHT - WINDOW,
        )
        base = pl.multiple_of(base, 16)
        bases.append(base)
        for p in range(PLANES):
            copy = pltpu.make_async_copy(
                x_ref.at[p // IMAGES, p % IMAGES, 0, pl.ds(base, WINDOW), :],
                win.at[side, p],
                sems.at[side, p],
            )
            copy.start()
            copies.append(copy)
    first_line, end_line = lines_ref[0, 0], lines_ref[0, 1]
    first_col, end_col = cols_ref[0, 0], cols_ref[0, 1]
    col = iota((1, SLANT_WIDTH), 1)
    inside = ((col >= first_col) & (col < end_col)).astype(F32).astype(BF16)
    curve = jnp.broadcast_to(curve_ref[...], (SENT, SWEEP_HEIGHT))
    outs = (a_ref, b_ref)
    for side in range(2):
        start = firsts[side]
        line = iota((SWEEP_HEIGHT, 128), 0)
        place = iota((SWEEP_HEIGHT, 128), 1)
        chosen = (
            (line == start + place)
            & (place < MARGIN)
            & (line >= first_line)
            & (line < end_line)
        )
        weights = jnp.dot(
            curve, chosen.astype(F32).astype(BF16), preferred_element_type=F32
        ).astype(BF16)
        row = iota((SENT, WINDOW), 0)
        source = iota((SENT, WINDOW), 1) + bases[side]
        pick = ((source == start + row) & (row < MARGIN)).astype(F32).astype(BF16)
        for p in range(PLANES):
            copies[side * PLANES + p].wait()
            for t in range(TILES):
                cols = slice(t * TILE, (t + 1) * TILE)
                block = jnp.dot(
                    pick, win[side, p, :, cols], preferred_element_type=F32
                ).astype(BF16)
                outs[side][p, :, cols] = block * inside[:, cols]
        head = outs[side][0, :, :128]
        last = iota((SENT, 128), 0) == MARGIN
        outs[side][0, :, :128] = jnp.where(last, weights, head)


def merge_kernel(
    start_ref,
    lines_ref,
    cols_ref,
    couples_ref,
    curve_ref,
    x_ref,
    a_ref,
    b_ref,
    ifg_ref,
    coh_ref,
    merged,
    acc,
    power,
):
    az = lax.axis_index("az")
    odd = lax.rem(az, 2)
    offset = line_offset(start_ref)
    slot = iota((BLOCK_HEIGHT, SWEEP_HEIGHT), 0)
    row = (slot & 7) * LOOK_ROWS + (slot >> 3)
    line = iota((BLOCK_HEIGHT, SWEEP_HEIGHT), 1)
    own = (line == row + offset) & (line >= lines_ref[0, 0]) & (line < lines_ref[0, 1])
    own = jnp.where(own, curve_ref[...].astype(F32), 0.0)

    def partner(ref, base):
        slot = iota((BLOCK_HEIGHT, SENT), 0)
        row = (slot & 7) * LOOK_ROWS + (slot >> 3)
        place = iota((BLOCK_HEIGHT, SENT), 1)
        weights = ref[0, MARGIN:SENT, :SENT].astype(F32)
        return jnp.where((row == base + place) & (place < MARGIN), weights, 0.0)

    above = BLOCK_HEIGHT - MARGIN
    side_a = partner(a_ref, jnp.where(odd == 1, 0, above))
    side_b = partner(b_ref, jnp.where(odd == 1, above, 0))
    select = jnp.concatenate([own, side_a, side_b], axis=1)
    total = jnp.sum(select, axis=1, keepdims=True)
    scale = jnp.broadcast_to(1.0 / total, (BLOCK_HEIGHT, TILE))
    select = select.astype(BF16)
    first_col, end_col = cols_ref[0, 0], cols_ref[0, 1]
    acc[...] = jnp.zeros_like(acc)

    def tile(t, carry):
        cols = pl.ds(pl.multiple_of(t * TILE, TILE), TILE)
        col = iota((1, TILE), 1) + t * TILE
        inside = ((col >= first_col) & (col < end_col)).astype(F32).astype(BF16)
        for p in range(PLANES):
            values = jnp.concatenate(
                [
                    x_ref[p // IMAGES, p % IMAGES, 0, :, cols] * inside,
                    a_ref[p, :, cols],
                    b_ref[p, :, cols],
                ],
                axis=0,
            )
            merged[p // IMAGES, p % IMAGES] = (
                jnp.dot(select, values, preferred_element_type=F32) * scale
            )

        def rows(v):
            return jnp.sum(v.reshape(LOOK_ROWS, BOXES, TILE), axis=0)

        real, imag, powers = [], [], []
        for p in range(PAIRS):
            i, j = couples_ref[p, 0], couples_ref[p, 1]
            ri, ii, rj, ij = merged[0, i], merged[1, i], merged[0, j], merged[1, j]
            real.append(rows(ri * rj + ii * ij))
            imag.append(rows(ii * rj - ri * ij))
        for a in range(IMAGES):
            powers.append(rows(merged[0, a] * merged[0, a] + merged[1, a] * merged[1, a]))
        sums = jnp.concatenate(real + imag + powers, axis=0)
        high = sums.astype(BF16)
        low = (sums - high.astype(F32)).astype(BF16)
        where = iota((TILE, LOOKS), 0) + t * TILE
        look = iota((TILE, LOOKS), 1) * LOOK_COLS
        box = ((where >= look) & (where < look + LOOK_COLS)).astype(F32).astype(BF16)
        acc[...] += jnp.dot(high, box, preferred_element_type=F32) + jnp.dot(
            low, box, preferred_element_type=F32
        )
        return carry

    lax.fori_loop(0, TILES, tile, 0)
    for a in range(IMAGES):
        power[a] = acc[(2 * PAIRS + a) * BOXES : (2 * PAIRS + a + 1) * BOXES, :]
    for p in range(PAIRS):
        re = acc[p * BOXES : (p + 1) * BOXES, :]
        im = acc[(PAIRS + p) * BOXES : (PAIRS + p + 1) * BOXES, :]
        ifg_ref[0, p] = re / float(LOOK_ROWS * LOOK_COLS)
        ifg_ref[1, p] = im / float(LOOK_ROWS * LOOK_COLS)
        both = power[couples_ref[p, 0]] * power[couples_ref[p, 1]]
        coh_ref[p] = (re * re + im * im) / jnp.maximum(both, 1.0)


def swaps(n, first):
    pairs = [(k, k + 1) for k in range(first, n - 1, 2)]
    return pairs + [(j, i) for i, j in pairs]


def per_device(
    sweep_stack,
    blend_curve,
    sweep_start_index,
    usable_azimuth_extent,
    usable_column_extent,
    image_couples,
):
    n = lax.axis_size("az")
    sent = pltpu.VMEM((PLANES, SENT, SLANT_WIDTH), BF16)
    in_hbm = pltpu.with_memory_space_constraint(sweep_stack, pltpu.HBM)
    to_a, to_b = pl.pallas_call(
        pack_kernel,
        out_shape=(sent, sent),
        in_specs=[SMEM, SMEM, SMEM, VMEM, HBM],
        out_specs=(VMEM, VMEM),
        scratch_shapes=[
            pltpu.VMEM((2, PLANES, WINDOW, SLANT_WIDTH), BF16),
            pltpu.SemaphoreType.DMA((2, PLANES)),
        ],
        compiler_params=pltpu.CompilerParams(vmem_limit_bytes=16 * 2**20),
        name="pack",
    )(sweep_start_index, usable_azimuth_extent, usable_column_extent, blend_curve, in_hbm)
    from_b = lax.ppermute(to_b, "az", swaps(n, 1))
    from_a = lax.ppermute(to_a, "az", swaps(n, 0))
    from_a = pltpu.with_memory_space_constraint(from_a, pltpu.VMEM)
    from_b = pltpu.with_memory_space_constraint(from_b, pltpu.VMEM)
    return pl.pallas_call(
        merge_kernel,
        out_shape=(
            jax.ShapeDtypeStruct((2, PAIRS, BOXES, LOOKS), F32),
            jax.ShapeDtypeStruct((PAIRS, BOXES, LOOKS), F32),
        ),
        in_specs=[SMEM, SMEM, SMEM, SMEM, VMEM, VMEM, VMEM, VMEM],
        out_specs=(VMEM, VMEM),
        scratch_shapes=[
            pltpu.VMEM((2, IMAGES, BLOCK_HEIGHT, TILE), F32),
            pltpu.VMEM((3 * PAIRS * BOXES, LOOKS), F32),
            pltpu.VMEM((IMAGES, BOXES, LOOKS), F32),
        ],
        compiler_params=pltpu.CompilerParams(vmem_limit_bytes=16 * 2**20),
        name="merge",
    )(
        sweep_start_index,
        usable_azimuth_extent,
        usable_column_extent,
        image_couples,
        blend_curve,
        sweep_stack,
        from_a,
        from_b,
    )


def solution(mesh):
    return jax.shard_map(
        per_device,
        mesh=mesh,
        in_specs=(
            P(None, None, ("groups", "az"), None, None),
            P(("groups", "az"), None),
            P(("groups", "az")),
            P(("groups", "az"), None),
            P(("groups", "az"), None),
            P("groups", None),
        ),
        out_specs=(P(None, "groups", "az", None), P("groups", "az", None)),
        check_vma=False,
    )
```

time: 84.3 us -> 48.1 us (0.57)
  local copies, waits for them, and re-layouts: 25.9 us -> 2.23 us
  other arithmetic: 22.1 us -> 0 us
  Pallas kernels: 0 us -> 11.6 us
  waiting for transfers between devices: 1.88 us -> 10.2 us
  starting transfers between devices: 29.7 us -> 22.5 us
  matrix products: 2.61 us -> 0 us
    gather x7 -> x0, local copies, waits for them, and re-layouts: 13.1 us -> none  [the longest x3 7.13 us: gather_lines(): chosen_indices = jnp.take(sweep_content, bounded_indices, axis=2)]
    pallas_call x0 -> x2, Pallas kernels: none -> 11.6 us  [the longest x1 6.56 us: per_device(): pl.pallas_call(merge_kernel, out_shape=(jax.ShapeDtypeStruct((2, PAIRS, B...]
    ppermute x4 -> x2, waiting for transfers between devices: 1.88 us -> 10.2 us  [the longest x1 10.2 us: per_device(): from_b = lax.ppermute(to_b, 'az', swaps(n, 1))]
    ppermute x4 -> x2, starting transfers between devices: 29.7 us -> 22.5 us  [the longest x1 20.5 us: per_device(): from_a = lax.ppermute(to_a, 'az', swaps(n, 0))]
    select_n x8 -> x0, other arithmetic: 5.96 us -> none  [the longest x1 3.01 us: gather_lines(): jnp.where(sample_valid, chosen_indices, jnp.zeros((), jnp.bfloat16))]
    unnamed x7 -> x17, local copies, waits for them, and re-layouts: 6.1 us -> 2.23 us
    reduce_sum x4 -> x0, other arithmetic: 3.66 us -> none  [the longest x2 3.3 us: looked(): aggregate = jnp.sum(shaped, axis=-2)]
    scatter-add x4 -> x0, other arithmetic: 3.44 us -> none  [the longest x1 1.64 us: per_device(): cross_term = cross_term.at[:, :, :extent_rows].add(from_below)]
  transfers between devices with their start and end apart: 4 -> 2, of which waited for: 1 -> 1; matrix products, arithmetic and copies ran while one was open for 26% -> 0% of each run, Pallas kernels for 0% -> 0%
where the time goes in v1:
time: 48.1 us; the launch traced here: 48 us
  starting transfers between devices  22.5 us (47%)
  Pallas kernels  11.6 us (24%)
  waiting for transfers between devices  10.2 us (21%)
  local copies, waits for them, and re-layouts  2.23 us (5%)
  between operations  1.49 us (3%)
    ppermute x1, starting transfers between devices, per_device(): from_a = lax.ppermute(to_a, 'az', swaps(n, 0))  20.5 us
    ppermute x1, waiting for transfers between devices, per_device(): from_b = lax.ppermute(to_b, 'az', swaps(n, 1))  10.2 us
    pallas_call x1, Pallas kernels, per_device(): pl.pallas_call(merge_kernel, out_shape=(jax.ShapeDtypeStruct((2, PAIRS, B...  6.56 us
    pallas_call x1, Pallas kernels, per_device(): pl.pallas_call(pack_kernel, out_shape=(sent, sent), in_specs=[SMEM, SMEM,...  5.03 us
    unnamed x17, local copies, waits for them, and re-layouts  2.23 us
    ppermute x1, starting transfers between devices, per_device(): from_b = lax.ppermute(to_b, 'az', swaps(n, 1))  1.94 us
  transfers between devices with their start and end apart: 2, of which 1 were waited for; matrix products, arithmetic and copies ran while one was open for 0% of the time, Pallas kernels for 0%

profile of v1, /device:TPU:37, one launch (start us, length us, event | category | flops | bytes accessed | tf_op | source)
XLA Modules:
  0.0 48.0 jit_solution(12762887940935116099)
XLA Ops:
  0.6 0.0 copy-start
  1.4 0.0 copy-start.1
  1.4 0.8 %copy-done.1 = s32[1,2]{1,0:T(1,128)S(1)} copy-done((s32[1,2]{1,0:T(1,128)S(1)}, s32[1,2]{1,0:T(1,128)}, u32[]{:S(2)}) %copy-start.1) | copy-done | bytes 32
  2.3 0.0 copy-start.3
  2.3 0.7 %copy-done.3 = s32[1,2]{1,0:T(1,128)S(1)} copy-done((s32[1,2]{1,0:T(1,128)S(1)}, s32[1,2]{1,0:T(1,128)}, u32[]{:S(2)}) %copy-start.3) | copy-done | bytes 32
  2.9 0.0 copy-start.5
  2.9 0.7 %copy-done.5 = bf16[1,80]{1,0:T(2,128)(2,1)S(1)} copy-done((bf16[1,80]{1,0:T(2,128)(2,1)S(1)}, bf16[1,80]{1,0:T(2,128)(2,1)}, u32[]{:S(2)}) %copy-start.5) | copy-done | bytes 184
  3.6 0.0 copy-start.7
  3.6 0.0 copy-start.2
  3.6 0.0 copy-start.4
  3.6 0.0 copy-start.6
  3.6 5.0 %pack.1 = (bf16[8,16,2560]{2,1,0:T(8,128)(2,1)}, bf16[8,16,2560]{2,1,0:T(8,128)(2,1)}) custom-call(s32[1]{0:T(128)S(6)} %copy.9.start_ref, s32[1,2]{1,0:T(1,128)S(1)} %copy-done.1, s32[1,2]{1,0:T(1,128)S(1)} %copy-done.3, bf16[1,80]{1,0:T(2,128)(2,1)S(1)} %copy-done.5, bf16[2,4,1,80,2560]{4,3,2,1,0:T(8,128)(2,1)} %x_ref.3), custom_call_target="tpu_custom_call" | custom-call | tf_op jit(solution)/shard_map/pack/pallas_call | solution.py:207
  8.6 20.5 %collective-permute-start = (bf16[8,16,2560]{2,1,0:T(8,128)(2,1)}, bf16[8,16,2560]{2,1,0:T(8,128)(2,1)}, u32[]{:S(2)}, u32[]{:S(2)}) collective-permute-start(bf16[8,16,2560]{2,1,0:T(8,128)(2,1)} %get-tuple-element.4), channel_id=1, source_target_pairs={{0,1},{2,3},{4,5},{6,7},{8,9},{10,11},{12,13},{14,15},{16,17},{18,... | collective-permute-start | bytes 1966088 | tf_op jit(solution)/shard_map/ppermute | solution.py:220
  29.1 1.9 %collective-permute-start.1 = (bf16[8,16,2560]{2,1,0:T(8,128)(2,1)}, bf16[8,16,2560]{2,1,0:T(8,128)(2,1)}, u32[]{:S(2)}, u32[]{:S(2)}) collective-permute-start(bf16[8,16,2560]{2,1,0:T(8,128)(2,1)} %get-tuple-element.5), channel_id=1, source_target_pairs={{1,2},{3,4},{5,6},{7,8},{9,10},{11,12},{13,14},{15,16},{17,18},{19... | collective-permute-start | bytes 1966088 | tf_op jit(solution)/shard_map/ppermute | solution.py:219
  31.1 0.0 copy-done.7
  31.1 0.1 copy.8.couples_ref
  31.2 0.0 collective-permute-done.a_ref
  31.2 10.2 %collective-permute-done.1.b_ref = bf16[8,16,2560]{2,1,0:T(8,128)(2,1)} collective-permute-done((bf16[8,16,2560]{2,1,0:T(8,128)(2,1)}, bf16[8,16,2560]{2,1,0:T(8,128)(2,1)}, u32[]{:S(2)}, u32[]{:S(2)}) %collective-permute-start.1) | collective-permute-done | bytes 655392 | tf_op jit(solution)/shard_map/ppermute | solution.py:219
  41.4 0.0 copy-done
  41.4 0.0 copy-done.2
  41.4 0.0 copy-done.4
  41.4 0.0 copy-done.6
  41.4 6.6 %merge.1 = (f32[2,4,8,128]{3,2,1,0:T(8,128)}, f32[4,8,128]{2,1,0:T(8,128)}) custom-call(s32[1]{0:T(128)S(6)} %copy.9.start_ref, s32[1,2]{1,0:T(1,128)S(1)} %copy-done.2, s32[1,2]{1,0:T(1,128)S(1)} %copy-done.4, s32[4,2]{1,0:T(4,128)S(1)} %copy.8.couples_ref, bf16[1,80]{1,0:T(2,128)(2,1)S(1)} %copy-done.6, bf16[2,4,1,80,2560]{4,3,2,1,0:T(8,128)(2,1)S(1)} %copy-done, ...), custom_call_target="tpu_custom_call" | custom-call | tf_op jit(solution)/shard_map/merge/pallas_call | solution.py:223
Async XLA Ops:
  0.6 40.8 %copy-start = (bf16[2,4,1,80,2560]{4,3,2,1,0:T(8,128)(2,1)S(1)}, bf16[2,4,1,80,2560]{4,3,2,1,0:T(8,128)(2,1)}, u32[]{:S(2)}) copy-start(bf16[2,4,1,80,2560]{4,3,2,1,0:T(8,128)(2,1)} %x_ref.3) | copy-start | bytes 9830404
  1.4 0.8 %copy-start.1 = (s32[1,2]{1,0:T(1,128)S(1)}, s32[1,2]{1,0:T(1,128)}, u32[]{:S(2)}) copy-start(s32[1,2]{1,0:T(1,128)} %lines_ref.3) | copy-start | bytes 28
  2.3 0.7 %copy-start.3 = (s32[1,2]{1,0:T(1,128)S(1)}, s32[1,2]{1,0:T(1,128)}, u32[]{:S(2)}) copy-start(s32[1,2]{1,0:T(1,128)} %cols_ref.3) | copy-start | bytes 28
  2.9 0.7 %copy-start.5 = (bf16[1,80]{1,0:T(2,128)(2,1)S(1)}, bf16[1,80]{1,0:T(2,128)(2,1)}, u32[]{:S(2)}) copy-start(bf16[1,80]{1,0:T(2,128)(2,1)} %curve_ref.3) | copy-start | bytes 484
  3.6 27.5 %copy-start.7 = (s32[4,2]{0,1:T(2,128)S(1)}, s32[4,2]{0,1:T(2,128)}, u32[]{:S(2)}) copy-start(s32[4,2]{0,1:T(2,128)} %param.11) | copy-start | bytes 100
  3.6 37.8 %copy-start.2 = (s32[1,2]{1,0:T(1,128)S(1)}, s32[1,2]{1,0:T(1,128)}, u32[]{:S(2)}) copy-start(s32[1,2]{1,0:T(1,128)} %lines_ref.3) | copy-start | bytes 28
  3.6 37.8 %copy-start.4 = (s32[1,2]{1,0:T(1,128)S(1)}, s32[1,2]{1,0:T(1,128)}, u32[]{:S(2)}) copy-start(s32[1,2]{1,0:T(1,128)} %cols_ref.3) | copy-start | bytes 28
  3.6 37.8 %copy-start.6 = (bf16[1,80]{1,0:T(2,128)(2,1)S(1)}, bf16[1,80]{1,0:T(2,128)(2,1)}, u32[]{:S(2)}) copy-start(bf16[1,80]{1,0:T(2,128)(2,1)} %curve_ref.3) | copy-start | bytes 484
  8.6 22.6 %collective-permute-start = (bf16[8,16,2560]{2,1,0:T(8,128)(2,1)}, bf16[8,16,2560]{2,1,0:T(8,128)(2,1)}, u32[]{:S(2)}, u32[]{:S(2)}) collective-permute-start(bf16[8,16,2560]{2,1,0:T(8,128)(2,1)} %get-tuple-element.4), channel_id=1, source_target_pairs={{0,1},{2,3},{4,5},{6,7},{8,9},{10,11},{12,13},{14,15},{16,17},{18,... | collective-permute-start | bytes 1966088 | tf_op jit(solution)/shard_map/ppermute | solution.py:220
  29.1 12.2 %collective-permute-start.1 = (bf16[8,16,2560]{2,1,0:T(8,128)(2,1)}, bf16[8,16,2560]{2,1,0:T(8,128)(2,1)}, u32[]{:S(2)}, u32[]{:S(2)}) collective-permute-start(bf16[8,16,2560]{2,1,0:T(8,128)(2,1)} %get-tuple-element.5), channel_id=1, source_target_pairs={{1,2},{3,4},{5,6},{7,8},{9,10},{11,12},{13,14},{15,16},{17,18},{19... | collective-permute-start | bytes 1966088 | tf_op jit(solution)/shard_map/ppermute | solution.py:219

commit v2 on v0

v2 whole, which is shorter than its diff:
```python
import functools

import jax
import jax.numpy as jnp
from jax import lax
from jax.experimental import pallas as pl
from jax.experimental.pallas import tpu as pltpu
from jax.sharding import PartitionSpec as P

BLOCK_HEIGHT = 40
SLANT_WIDTH = 2560
LOOK_ROWS = 5
LOOK_COLS = 20
MARGIN = 15
SWEEP_HEIGHT = 80
IMAGES = 4
PLANES = 2 * IMAGES
PAIRS = 4
SENT = 16
WINDOW = 32
LOOKS = SLANT_WIDTH // LOOK_COLS
BOXES = BLOCK_HEIGHT // LOOK_ROWS
EDGE_BOXES = MARGIN // LOOK_ROWS
SUMS = (2 * PAIRS + IMAGES) * BOXES
TILE = 256
TILES = SLANT_WIDTH // TILE
HALF = SLANT_WIDTH // 2
F32 = jnp.float32
BF16 = jnp.bfloat16

HBM = pl.BlockSpec(memory_space=pltpu.HBM)
VMEM = pl.BlockSpec(memory_space=pltpu.VMEM)
SMEM = pl.BlockSpec(memory_space=pltpu.SMEM)


def iota(shape, dim):
    return lax.broadcasted_iota(jnp.int32, shape, dim)


def as_bf16(mask):
    return mask.astype(F32).astype(BF16)


def position():
    az = lax.axis_index("az")
    return az, lax.rem(az, 2) == 1


def columns_inside(cols_ref, first, count):
    col = iota((1, count), 1) + first
    return as_bf16((col >= cols_ref[0, 0]) & (col < cols_ref[0, 1]))


def take_lines(first, x_plane, lines_ref, cols_ref, curve_ref, out_ref):
    base = lax.shift_left(lax.shift_right_arithmetic(first, 4), 4)
    base = pl.multiple_of(jnp.clip(base, 0, SWEEP_HEIGHT - WINDOW), 16)
    line = iota((SWEEP_HEIGHT, 128), 0)
    place = iota((SWEEP_HEIGHT, 128), 1)
    chosen = (
        (line == first + place)
        & (place < MARGIN)
        & (line >= lines_ref[0, 0])
        & (line < lines_ref[0, 1])
    )
    curve = jnp.broadcast_to(curve_ref[...], (SENT, SWEEP_HEIGHT))
    weights = jnp.dot(curve, as_bf16(chosen), preferred_element_type=F32).astype(BF16)
    row = iota((SENT, WINDOW), 0)
    source = iota((SENT, WINDOW), 1) + base
    pick = as_bf16((source == first + row) & (row < MARGIN))
    inside = columns_inside(cols_ref, 0, SLANT_WIDTH)
    for p in range(PLANES):
        window = x_plane(p)
        for t in range(TILES):
            cols = slice(t * TILE, (t + 1) * TILE)
            block = jnp.dot(pick, window[pl.ds(base, WINDOW), cols], preferred_element_type=F32)
            out_ref[p, :, cols] = block.astype(BF16) * inside[:, cols]
    last = iota((SENT, 128), 0) == MARGIN
    out_ref[0, :, :128] = jnp.where(last, weights, out_ref[0, :, :128])


def pack_kernel(
    start_ref,
    lines_hbm,
    cols_hbm,
    curve_hbm,
    x_hbm,
    a_ref,
    b_ref,
    x,
    lines_ref,
    cols_ref,
    curve_ref,
    sems,
    small_sems,
):
    small = (
        pltpu.make_async_copy(lines_hbm, lines_ref, small_sems.at[0]),
        pltpu.make_async_copy(cols_hbm, cols_ref, small_sems.at[1]),
        pltpu.make_async_copy(curve_hbm, curve_ref, small_sems.at[2]),
    )
    for copy in small:
        copy.start()
    planes = [
        pltpu.make_async_copy(x_hbm.at[p // IMAGES, p % IMAGES, 0], x.at[p], sems.at[p])
        for p in range(PLANES)
    ]
    for copy in planes:
        copy.start()
    for copy in small:
        copy.wait()
    az, odd = position()
    offset = az * BLOCK_HEIGHT - start_ref[0]
    down = offset - MARGIN
    up = offset + BLOCK_HEIGHT

    def arriving(p):
        planes[p].wait()
        return x.at[p]

    take_lines(jnp.where(odd, down, up), arriving, lines_ref, cols_ref, curve_ref, a_ref)

    @pl.when((az > 0) & (az < lax.axis_size("az") - 1))
    def _():
        take_lines(jnp.where(odd, up, down), x.at.__getitem__, lines_ref, cols_ref, curve_ref, b_ref)


def reciprocal(total):
    return jnp.where(total > 0.0, 1.0 / total, 0.0)


def look_sums(merged, couples_ref, box):
    def rows(v):
        return jnp.sum(v.reshape(LOOK_ROWS, BOXES, TILE), axis=0)

    real, imag, powers = [], [], []
    for p in range(PAIRS):
        i, j = couples_ref[p, 0], couples_ref[p, 1]
        ri, ii, rj, ij = merged[0, i], merged[1, i], merged[0, j], merged[1, j]
        real.append(rows(ri * rj + ii * ij))
        imag.append(rows(ii * rj - ri * ij))
    for a in range(IMAGES):
        re, im = merged[0, a], merged[1, a]
        powers.append(rows(re * re + im * im))
    sums = jnp.concatenate(real + imag + powers, axis=0)
    high = sums.astype(BF16)
    low = (sums - high.astype(F32)).astype(BF16)
    return jnp.dot(high, box, preferred_element_type=F32) + jnp.dot(
        low, box, preferred_element_type=F32
    )


def look_box(first):
    where = iota((TILE, LOOKS), 0) + first
    look = iota((TILE, LOOKS), 1) * LOOK_COLS
    return as_bf16((where >= look) & (where < look + LOOK_COLS))


def partner_weights(ref):
    return ref[0, MARGIN:SENT, :SENT].astype(F32)


def own_kernel(
    late,
    start_ref,
    lines_ref,
    cols_ref,
    couples_ref,
    curve_ref,
    x_hbm,
    b_ref,
    *rest,
):
    lines_out, sums_out, x, merged, sem = rest[-5:]
    az, odd = position()

    @pl.when((az == 0) if late else (az > 0))
    def _():
        copy = pltpu.make_async_copy(x_hbm, x, sem)
        copy.start()
        copy.wait()
        offset = az * BLOCK_HEIGHT - start_ref[0]
        above = BLOCK_HEIGHT - MARGIN
        first = offset + jnp.where(odd, 0, above)
        take_lines(
            first,
            lambda p: x.at[p // IMAGES, p % IMAGES, 0],
            lines_ref,
            cols_ref,
            curve_ref,
            lines_out,
        )
        slot = iota((BLOCK_HEIGHT, SWEEP_HEIGHT), 0)
        row = (slot & 7) * LOOK_ROWS + (slot >> 3)
        line = iota((BLOCK_HEIGHT, SWEEP_HEIGHT), 1)
        own = (line == row + offset) & (line >= lines_ref[0, 0]) & (line < lines_ref[0, 1])
        own = jnp.where(own, curve_ref[...].astype(F32), 0.0)
        slot = iota((BLOCK_HEIGHT, SENT), 0)
        row = (slot & 7) * LOOK_ROWS + (slot >> 3)
        place = iota((BLOCK_HEIGHT, SENT), 1)
        match = (row == place + jnp.where(odd, above, 0)) & (place < MARGIN)
        other = jnp.where(match, partner_weights(b_ref), 0.0)
        select = jnp.concatenate([own, other], axis=1)
        total = jnp.sum(select, axis=1, keepdims=True)
        scale = jnp.broadcast_to(reciprocal(total), (BLOCK_HEIGHT, TILE))
        select = select.astype(BF16)
        sums_out[...] = jnp.zeros_like(sums_out)

        def two_tiles(k, carry):
            for u in range(2):
                begin = pl.multiple_of((k * 2 + u) * TILE, TILE)
                cols = pl.ds(begin, TILE)
                inside = columns_inside(cols_ref, begin, TILE)
                for p in range(PLANES):
                    c, a = p // IMAGES, p % IMAGES
                    values = jnp.concatenate(
                        [x[c, a, 0, :, cols] * inside, b_ref[p, :, cols]], axis=0
                    )
                    merged[u, c, a] = (
                        jnp.dot(select, values, preferred_element_type=F32) * scale
                    )
            sums = [
                look_sums(merged.at[u], couples_ref, look_box((k * 2 + u) * TILE))
                for u in range(2)
            ]
            sums_out[...] += sums[0] + sums[1]
            return carry

        lax.fori_loop(0, TILES // 2, two_tiles, 0)


def edge_kernel(couples_ref, a_ref, own_ref, sums_ref, ifg_ref, coh_ref, merged, acc, power):
    _, odd = position()
    slot = iota((BLOCK_HEIGHT, SENT), 0)
    place = iota((BLOCK_HEIGHT, SENT), 1)
    edge = slot & 3
    match = (place == edge * LOOK_ROWS + (slot >> 3)) & (edge < EDGE_BOXES)
    lower = (slot & 4) == 0
    theirs = jnp.where(match, partner_weights(a_ref), 0.0)
    ours = jnp.where(match, partner_weights(own_ref), 0.0)
    total = jnp.sum(theirs + ours, axis=1, keepdims=True)
    scale = jnp.broadcast_to(reciprocal(total), (BLOCK_HEIGHT, TILE))
    select = jnp.concatenate(
        [
            jnp.where(lower, theirs, 0.0),
            jnp.where(lower, ours, 0.0),
            jnp.where(lower, 0.0, theirs),
            jnp.where(lower, 0.0, ours),
        ],
        axis=1,
    ).astype(BF16)
    total = None
    for t in range(HALF // TILE):
        one = slice(t * TILE, (t + 1) * TILE)
        two = slice(HALF + t * TILE, HALF + (t + 1) * TILE)
        for p in range(PLANES):
            values = jnp.concatenate(
                [a_ref[p, :, one], own_ref[p, :, one], a_ref[p, :, two], own_ref[p, :, two]],
                axis=0,
            )
            merged[t, p // IMAGES, p % IMAGES] = (
                jnp.dot(select, values, preferred_element_type=F32) * scale
            )
        part = look_sums(merged.at[t], couples_ref, look_box(t * TILE))
        total = part if total is None else total + part
    acc[...] = total
    sublane = iota((BOXES, LOOKS), 0)
    lane = iota((BOXES, LOOKS), 1)
    lowest = jnp.where(odd, 0, BOXES - EDGE_BOXES)
    mine = (sublane >= lowest) & (sublane < lowest + EDGE_BOXES)

    def whole(u):
        part = acc[u * BOXES : (u + 1) * BOXES, :]
        upper = pltpu.roll(pltpu.roll(part, LOOKS // 2, 1), 4, 0)
        part = jnp.where(lane < LOOKS // 2, part, upper)
        part = jnp.where(odd, part, pltpu.roll(part, BOXES - EDGE_BOXES, 0))
        return jnp.where(mine, part, sums_ref[u * BOXES : (u + 1) * BOXES, :])

    for a in range(IMAGES):
        power[a] = whole(2 * PAIRS + a)
    for p in range(PAIRS):
        re = whole(p)
        im = whole(PAIRS + p)
        ifg_ref[0, p] = re / float(LOOK_ROWS * LOOK_COLS)
        ifg_ref[1, p] = im / float(LOOK_ROWS * LOOK_COLS)
        both = power[couples_ref[p, 0]] * power[couples_ref[p, 1]]
        coh_ref[p] = (re * re + im * im) / jnp.maximum(both, 1.0)


def swaps(n, first):
    pairs = [(k, k + 1) for k in range(first, n - 1, 2)]
    return pairs + [(j, i) for i, j in pairs]


def limit(mebibytes):
    return pltpu.CompilerParams(vmem_limit_bytes=mebibytes * 2**20)


def in_hbm(array):
    return pltpu.with_memory_space_constraint(array, pltpu.HBM)


def per_device(
    sweep_stack,
    blend_curve,
    sweep_start_index,
    usable_azimuth_extent,
    usable_column_extent,
    image_couples,
):
    n = lax.axis_size("az")
    sent = jax.ShapeDtypeStruct((PLANES, SENT, SLANT_WIDTH), BF16)
    small = (sweep_start_index, usable_azimuth_extent, usable_column_extent)
    to_a, to_b = pl.pallas_call(
        pack_kernel,
        out_shape=(sent, sent),
        in_specs=[SMEM] + [HBM] * 4,
        out_specs=(VMEM, VMEM),
        scratch_shapes=[
            pltpu.VMEM((PLANES, SWEEP_HEIGHT, SLANT_WIDTH), BF16),
            pltpu.SMEM((1, 2), jnp.int32),
            pltpu.SMEM((1, 2), jnp.int32),
            pltpu.VMEM((1, SWEEP_HEIGHT), BF16),
            pltpu.SemaphoreType.DMA((PLANES,)),
            pltpu.SemaphoreType.DMA((3,)),
        ],
        compiler_params=limit(16),
        name="pack",
    )(small[0], *(in_hbm(array) for array in (*small[1:], blend_curve, sweep_stack)))
    from_b = lax.ppermute(to_b, "az", swaps(n, 1))
    from_a = lax.ppermute(to_a, "az", swaps(n, 0))

    def own(late, *before):
        operands = (*small, image_couples, blend_curve, in_hbm(sweep_stack), from_b, *before)
        return pl.pallas_call(
            functools.partial(own_kernel, late),
            out_shape=(sent, jax.ShapeDtypeStruct((SUMS, LOOKS), F32)),
            in_specs=[SMEM] * 4 + [VMEM, HBM, VMEM] + [VMEM] * len(before),
            out_specs=(VMEM, VMEM),
            scratch_shapes=[
                pltpu.VMEM((2, IMAGES, 1, SWEEP_HEIGHT, SLANT_WIDTH), BF16),
                pltpu.VMEM((2, 2, IMAGES, BLOCK_HEIGHT, TILE), F32),
                pltpu.SemaphoreType.DMA,
            ],
            input_output_aliases={7: 0, 8: 1} if before else {},
            compiler_params=limit(16),
            name="late" if late else "early",
        )(*operands)

    lines, sums = own(False)
    lines, sums = own(True, lines, sums)
    return pl.pallas_call(
        edge_kernel,
        out_shape=(
            jax.ShapeDtypeStruct((2, PAIRS, BOXES, LOOKS), F32),
            jax.ShapeDtypeStruct((PAIRS, BOXES, LOOKS), F32),
        ),
        in_specs=[SMEM, VMEM, VMEM, VMEM],
        out_specs=(VMEM, VMEM),
        scratch_shapes=[
            pltpu.VMEM((HALF // TILE, 2, IMAGES, BLOCK_HEIGHT, TILE), F32),
            pltpu.VMEM((SUMS, LOOKS), F32),
            pltpu.VMEM((IMAGES, BOXES, LOOKS), F32),
        ],
        compiler_params=limit(16),
        name="edge",
    )(image_couples, from_a, lines, sums)


def solution(mesh):
    return jax.shard_map(
        per_device,
        mesh=mesh,
        in_specs=(
            P(None, None, ("groups", "az"), None, None),
            P(("groups", "az"), None),
            P(("groups", "az")),
            P(("groups", "az"), None),
            P(("groups", "az"), None),
            P("groups", None),
        ),
        out_specs=(P(None, "groups", "az", None), P("groups", "az", None)),
        check_vma=False,
    )
```

time: 84.3 us -> 35.4 us (0.42)
  local copies, waits for them, and re-layouts: 25.9 us -> 0.11 us
  other arithmetic: 22.1 us -> 0 us
  Pallas kernels: 0 us -> 12.8 us
  starting transfers between devices: 29.7 us -> 20.9 us
  matrix products: 2.61 us -> 0 us
  waiting for transfers between devices: 1.88 us -> 0.01 us
    gather x7 -> x0, local copies, waits for them, and re-layouts: 13.1 us -> none  [the longest x3 7.13 us: gather_lines(): chosen_indices = jnp.take(sweep_content, bounded_indices, axis=2)]
    pallas_call x0 -> x4, Pallas kernels: none -> 12.8 us  [the longest x2 6.51 us: own(): pl.pallas_call(functools.partial(own_kernel, late), out_shape=(sent, jax....]
    ppermute x4 -> x2, starting transfers between devices: 29.7 us -> 20.9 us  [the longest x1 15.8 us: per_device(): from_a = lax.ppermute(to_a, 'az', swaps(n, 0))]
    unnamed x7 -> x9, local copies, waits for them, and re-layouts: 6.1 us -> 0.11 us
    select_n x8 -> x0, other arithmetic: 5.96 us -> none  [the longest x1 3.01 us: gather_lines(): jnp.where(sample_valid, chosen_indices, jnp.zeros((), jnp.bfloat16))]
    reduce_sum x4 -> x0, other arithmetic: 3.66 us -> none  [the longest x2 3.3 us: looked(): aggregate = jnp.sum(shaped, axis=-2)]
    scatter-add x4 -> x0, other arithmetic: 3.44 us -> none  [the longest x1 1.64 us: per_device(): cross_term = cross_term.at[:, :, :extent_rows].add(from_below)]
    slice x2 -> x0, local copies, waits for them, and re-layouts: 2.69 us -> none  [the longest x1 1.38 us: per_device(): usable_azimuth_extent[0, 0]]
  transfers between devices with their start and end apart: 4 -> 2, of which waited for: 1 -> 0; matrix products, arithmetic and copies ran while one was open for 26% -> 0% of each run, Pallas kernels for 0% -> 19%
where the time goes in v2:
time: 35.4 us; the launch traced here: 35.2 us
  starting transfers between devices  20.9 us (59%)
  Pallas kernels  12.8 us (36%)
  between operations  1.39 us (4%)
    ppermute x1, starting transfers between devices, per_device(): from_a = lax.ppermute(to_a, 'az', swaps(n, 0))  15.8 us
    pallas_call x2, Pallas kernels, own(): pl.pallas_call(functools.partial(own_kernel, late), out_shape=(sent, jax....  6.51 us
    ppermute x1, starting transfers between devices, per_device(): from_b = lax.ppermute(to_b, 'az', swaps(n, 1))  5.09 us
    pallas_call x1, Pallas kernels, per_device(): pl.pallas_call(pack_kernel, out_shape=(sent, sent), in_specs=[SMEM] + [HB...  3.33 us
    pallas_call x1, Pallas kernels, per_device(): pl.pallas_call(edge_kernel, out_shape=(jax.ShapeDtypeStruct((2, PAIRS, BO...  2.98 us
  transfers between devices with their start and end apart: 2, of which 0 were waited for; matrix products, arithmetic and copies ran while one was open for 0% of the time, Pallas kernels for 19%

profile of v2, /device:TPU:37, one launch (start us, length us, event | category | flops | bytes accessed | tf_op | source)
XLA Modules:
  0.0 35.2 jit_solution(6964092046756952227)
XLA Ops:
  0.6 0.0 copy-start.1
  0.6 0.0 copy-start
  0.7 0.0 copy-start.2
  0.7 0.0 copy-start.3
  1.3 3.3 %pack.1 = (bf16[8,16,2560]{2,1,0:T(8,128)(2,1)S(1)}, bf16[8,16,2560]{2,1,0:T(8,128)(2,1)S(1)}) custom-call(s32[1]{0:T(128)S(6)} %copy.15.start_ref, s32[1,2]{1,0:T(1,128)} %lines_ref.3, s32[1,2]{1,0:T(1,128)} %cols_ref.3, bf16[1,80]{1,0:T(2,128)(2,1)} %curve_ref.3, bf16[2,4,1,80,2560]{4,3,2,1,0:T(8,128)(2,1)} %x_hbm.5), custom_call_target="tpu_custom_call" | custom-call | tf_op jit(solution)/shard_map/pack/pallas_call | solution.py:313
  4.7 5.1 %collective-permute-start.1 = (bf16[8,16,2560]{2,1,0:T(8,128)(2,1)S(1)}, bf16[8,16,2560]{2,1,0:T(8,128)(2,1)S(1)}, u32[]{:S(2)}, u32[]{:S(2)}) collective-permute-start(bf16[8,16,2560]{2,1,0:T(8,128)(2,1)S(1)} %get-tuple-element.9), channel_id=1, source_target_pairs={{1,2},{3,4},{5,6},{7,8},{9,10},{11,12},{13,14},{15,16},{17,18},{19... | collective-permute-start | bytes 1966088 | tf_op jit(solution)/shard_map/ppermute | solution.py:329
  9.8 15.8 %collective-permute-start = (bf16[8,16,2560]{2,1,0:T(8,128)(2,1)S(1)}, bf16[8,16,2560]{2,1,0:T(8,128)(2,1)S(1)}, u32[]{:S(2)}, u32[]{:S(2)}) collective-permute-start(bf16[8,16,2560]{2,1,0:T(8,128)(2,1)S(1)} %get-tuple-element.8), channel_id=1, source_target_pairs={{0,1},{2,3},{4,5},{6,7},{8,9},{10,11},{12,13},{14,15},{16,17},{18,... | collective-permute-start | bytes 1966088 | tf_op jit(solution)/shard_map/ppermute | solution.py:330
  25.6 0.0 copy-done.3
  25.6 0.1 copy.12.couples_ref
  25.7 0.0 collective-permute-done.1.b_ref
  25.7 0.0 copy-done.1
  25.7 0.0 copy-done
  25.7 0.0 copy-done.2
  25.7 5.9 %early.1 = (bf16[8,16,2560]{2,1,0:T(8,128)(2,1)S(1)}, f32[96,128]{1,0:T(8,128)S(1)}) custom-call(s32[1]{0:T(128)S(6)} %copy.15.start_ref, s32[1,2]{1,0:T(1,128)S(1)} %copy-done, s32[1,2]{1,0:T(1,128)S(1)} %copy-done.1, s32[4,2]{1,0:T(4,128)S(1)} %copy.12.couples_ref, bf16[1,80]{1,0:T(2,128)(2,1)S(1)} %copy-done.2, bf16[2,4,1,80,2560]{4,3,2,1,0:T(8,128)(2,1)} %x_hbm.5, ...), custom_call_target="tpu_custom_call" | custom-call | tf_op jit(solution)/shard_map/early/pallas_call | solution.py:334
  31.6 0.6 %late.1 = (bf16[8,16,2560]{2,1,0:T(8,128)(2,1)S(1)}, f32[96,128]{1,0:T(8,128)S(1)}) custom-call(s32[1]{0:T(128)S(6)} %copy.15.start_ref, s32[1,2]{1,0:T(1,128)S(1)} %copy-done, s32[1,2]{1,0:T(1,128)S(1)} %copy-done.1, s32[4,2]{1,0:T(4,128)S(1)} %copy.12.couples_ref, bf16[1,80]{1,0:T(2,128)(2,1)S(1)} %copy-done.2, ...), custom_call_target="tpu_custom_call", output_to_operand_aliasing={{0}: (7, {}), {1}: (8, {})} | custom-call | tf_op jit(solution)/shard_map/late/pallas_call | solution.py:334
  32.2 0.0 collective-permute-done.a_ref
  32.3 3.0 %edge.1 = (f32[2,4,8,128]{3,2,1,0:T(8,128)}, f32[4,8,128]{2,1,0:T(8,128)}) custom-call(s32[4,2]{1,0:T(4,128)S(1)} %copy.12.couples_ref, bf16[8,16,2560]{2,1,0:T(8,128)(2,1)S(1)} %collective-permute-done.a_ref, bf16[8,16,2560]{2,1,0:T(8,128)(2,1)S(1)} %get-tuple-element.12.own_ref, f32[96,128]{1,0:T(8,128)S(1)} %get-tuple-element.13.sums_ref), custom_call_target="tpu_custom_call" | custom-call | tf_op jit(solution)/shard_map/edge/pallas_call | solution.py:351
Async XLA Ops:
  0.6 25.1 %copy-start.1 = (s32[1,2]{1,0:T(1,128)S(1)}, s32[1,2]{1,0:T(1,128)}, u32[]{:S(2)}) copy-start(s32[1,2]{1,0:T(1,128)} %cols_ref.3) | copy-start | bytes 28
  0.6 25.1 %copy-start = (s32[1,2]{1,0:T(1,128)S(1)}, s32[1,2]{1,0:T(1,128)}, u32[]{:S(2)}) copy-start(s32[1,2]{1,0:T(1,128)} %lines_ref.3) | copy-start | bytes 28
  0.7 25.1 %copy-start.2 = (bf16[1,80]{1,0:T(2,128)(2,1)S(1)}, bf16[1,80]{1,0:T(2,128)(2,1)}, u32[]{:S(2)}) copy-start(bf16[1,80]{1,0:T(2,128)(2,1)} %curve_ref.3) | copy-start | bytes 484
  0.7 24.9 %copy-start.3 = (s32[4,2]{0,1:T(2,128)S(1)}, s32[4,2]{0,1:T(2,128)}, u32[]{:S(2)}) copy-start(s32[4,2]{0,1:T(2,128)} %param.11) | copy-start | bytes 100
  4.7 21.0 %collective-permute-start.1 = (bf16[8,16,2560]{2,1,0:T(8,128)(2,1)S(1)}, bf16[8,16,2560]{2,1,0:T(8,128)(2,1)S(1)}, u32[]{:S(2)}, u32[]{:S(2)}) collective-permute-start(bf16[8,16,2560]{2,1,0:T(8,128)(2,1)S(1)} %get-tuple-element.9), channel_id=1, source_target_pairs={{1,2},{3,4},{5,6},{7,8},{9,10},{11,12},{13,14},{15,16},{17,18},{19... | collective-permute-start | bytes 1966088 | tf_op jit(solution)/shard_map/ppermute | solution.py:329
  9.8 22.5 %collective-permute-start = (bf16[8,16,2560]{2,1,0:T(8,128)(2,1)S(1)}, bf16[8,16,2560]{2,1,0:T(8,128)(2,1)S(1)}, u32[]{:S(2)}, u32[]{:S(2)}) collective-permute-start(bf16[8,16,2560]{2,1,0:T(8,128)(2,1)S(1)} %get-tuple-element.8), channel_id=1, source_target_pairs={{0,1},{2,3},{4,5},{6,7},{8,9},{10,11},{12,13},{14,15},{16,17},{18,... | collective-permute-start | bytes 1966088 | tf_op jit(solution)/shard_map/ppermute | solution.py:330

commit v3 on v2

v3 whole, which is shorter than its diff:
```python
import functools

import jax
import jax.numpy as jnp
from jax import lax
from jax.experimental import pallas as pl
from jax.experimental.pallas import tpu as pltpu
from jax.sharding import PartitionSpec as P

BLOCK_HEIGHT = 40
SLANT_WIDTH = 2560
LOOK_ROWS = 5
LOOK_COLS = 20
MARGIN = 15
SWEEP_HEIGHT = 80
IMAGES = 4
PLANES = 2 * IMAGES
PAIRS = 4
SENT = 16
WINDOW = 32
LOOKS = SLANT_WIDTH // LOOK_COLS
BOXES = BLOCK_HEIGHT // LOOK_ROWS
TILE = 256
TILES = SLANT_WIDTH // TILE
F32 = jnp.float32
BF16 = jnp.bfloat16

HBM = pl.BlockSpec(memory_space=pltpu.HBM)
VMEM = pl.BlockSpec(memory_space=pltpu.VMEM)
SMEM = pl.BlockSpec(memory_space=pltpu.SMEM)


def iota(shape, dim):
    return lax.broadcasted_iota(jnp.int32, shape, dim)


def as_bf16(mask):
    return mask.astype(F32).astype(BF16)


def position():
    az = lax.axis_index("az")
    return az, lax.rem(az, 2) == 1


def columns_inside(cols_ref, first, count):
    col = iota((1, count), 1) + first
    return as_bf16((col >= cols_ref[0, 0]) & (col < cols_ref[0, 1]))


def window_base(first):
    base = lax.shift_left(lax.shift_right_arithmetic(first, 4), 4)
    return pl.multiple_of(jnp.clip(base, 0, SWEEP_HEIGHT - WINDOW), 16)


def take_lines(first, base, window, lines_ref, cols_ref, curve_ref, out_ref):
    line = iota((SWEEP_HEIGHT, 128), 0)
    place = iota((SWEEP_HEIGHT, 128), 1)
    chosen = (
        (line == first + place)
        & (place < MARGIN)
        & (line >= lines_ref[0, 0])
        & (line < lines_ref[0, 1])
    )
    curve = jnp.broadcast_to(curve_ref[...], (SENT, SWEEP_HEIGHT))
    weights = jnp.dot(curve, as_bf16(chosen), preferred_element_type=F32).astype(BF16)
    row = iota((SENT, WINDOW), 0)
    source = iota((SENT, WINDOW), 1) + base
    pick = as_bf16((source == first + row) & (row < MARGIN))
    inside = columns_inside(cols_ref, 0, SLANT_WIDTH)
    for p in range(PLANES):
        lines = window(p)
        for t in range(TILES):
            cols = slice(t * TILE, (t + 1) * TILE)
            block = jnp.dot(pick, lines[:, cols], preferred_element_type=F32)
            out_ref[p, :, cols] = block.astype(BF16) * inside[:, cols]
    last = iota((SENT, 128), 0) == MARGIN
    out_ref[0, :, :128] = jnp.where(last, weights, out_ref[0, :, :128])


def start_all(*pairs):
    copies = [pltpu.make_async_copy(source, target, sem) for source, target, sem in pairs]
    for copy in copies:
        copy.start()
    return copies


def wait_all(copies):
    for copy in copies:
        copy.wait()


def pack_kernel(
    start_ref,
    lines_hbm,
    cols_hbm,
    curve_hbm,
    x_hbm,
    a_ref,
    b_ref,
    windows,
    lines_ref,
    cols_ref,
    curve_ref,
    sems,
    small_sems,
):
    az, odd = position()
    offset = az * BLOCK_HEIGHT - start_ref[0]
    down = offset - MARGIN
    up = offset + BLOCK_HEIGHT
    firsts = (jnp.where(odd, down, up), jnp.where(odd, up, down))
    bases = [window_base(first) for first in firsts]

    def fetch(side):
        rows = pl.ds(bases[side], WINDOW)
        return start_all(
            *(
                (
                    x_hbm.at[p // IMAGES, p % IMAGES, 0, rows, :],
                    windows.at[side, p],
                    sems.at[side, p],
                )
                for p in range(PLANES)
            )
        )

    near = fetch(0)
    small = start_all(
        (lines_hbm, lines_ref, small_sems.at[0]),
        (cols_hbm, cols_ref, small_sems.at[1]),
        (curve_hbm, curve_ref, small_sems.at[2]),
    )
    wait_all(small)

    def take(side, copies, out_ref):
        def window(p):
            copies[p].wait()
            return windows.at[side, p]

        take_lines(firsts[side], bases[side], window, lines_ref, cols_ref, curve_ref, out_ref)

    take(0, near, a_ref)

    @pl.when((az > 0) & (az < lax.axis_size("az") - 1))
    def _():
        take(1, fetch(1), b_ref)


def weights_of(ref):
    return ref[0, MARGIN:SENT, :SENT].astype(F32)


def box_sums(parts, boxes, sources, couples_ref, merged_refs, ready=None):
    stride = BOXES // parts
    width = SLANT_WIDTH // parts
    slot = iota((BLOCK_HEIGHT, SENT), 0)
    place = iota((BLOCK_HEIGHT, SENT), 1)
    box = slot & (stride - 1)
    part = (slot & 7) // stride
    match = (place == box * LOOK_ROWS + (slot >> 3)) & (box < boxes)
    chosen = [jnp.where(match, weights_of(ref), 0.0) for ref in sources]
    total = jnp.sum(sum(chosen), axis=1, keepdims=True)
    scale = jnp.where(total > 0.0, 1.0 / total, 0.0)
    scale = jnp.broadcast_to(scale, (BLOCK_HEIGHT, TILE))
    select = jnp.concatenate(
        [jnp.where(part == q, w, 0.0) for q in range(parts) for w in chosen], axis=1
    ).astype(BF16)
    tiles = [(at, min(TILE, width - at)) for at in range(0, width, TILE)]
    for (at, size), merged in zip(tiles, merged_refs):
        for p in range(PLANES):
            values = jnp.concatenate(
                [
                    ref[p, :, q * width + at : q * width + at + size]
                    for q in range(parts)
                    for ref in sources
                ],
                axis=0,
            )
            merged[p // IMAGES, p % IMAGES, :, :size] = (
                jnp.dot(select, values, preferred_element_type=F32) * scale[:, :size]
            )
    if ready is not None:
        ready()
    couples = [(couples_ref[p, 0], couples_ref[p, 1]) for p in range(PAIRS)]
    acc = None
    for (at, size), merged in zip(tiles, merged_refs):

        def rows(v):
            return jnp.sum(v.reshape(LOOK_ROWS, BOXES, size), axis=0)

        def plane(c, image):
            return merged[c, image, :, :size]

        real, imag, powers = [], [], []
        for i, j in couples:
            ri, ii, rj, ij = plane(0, i), plane(1, i), plane(0, j), plane(1, j)
            real.append(rows(ri * rj + ii * ij))
            imag.append(rows(ii * rj - ri * ij))
        for a in range(IMAGES):
            re, im = plane(0, a), plane(1, a)
            powers.append(rows(re * re + im * im))
        sums = jnp.concatenate(real + imag + powers, axis=0)
        high = sums.astype(BF16)
        low = (sums - high.astype(F32)).astype(BF16)
        where = iota((size, LOOKS), 0) + at
        look = iota((size, LOOKS), 1) * LOOK_COLS
        cells = as_bf16((where >= look) & (where < look + LOOK_COLS))
        got = jnp.dot(high, cells, preferred_element_type=F32) + jnp.dot(
            low, cells, preferred_element_type=F32
        )
        acc = got if acc is None else acc + got
    lane = iota((BOXES, LOOKS), 1)
    step = LOOKS // parts
    out = []
    for u in range(3 * PAIRS):
        got = acc[u * BOXES : (u + 1) * BOXES, :]
        whole = got
        for q in range(1, parts):
            moved = pltpu.roll(pltpu.roll(got, q * step, 1), BOXES - q * stride, 0)
            whole = jnp.where(lane >= q * step, moved, whole)
        out.append(whole)
    return out


def own_kernel(
    late,
    start_ref,
    lines_hbm,
    cols_hbm,
    couples_hbm,
    curve_hbm,
    x_hbm,
    *rest,
):
    (
        a_out,
        b_out,
        sums_out,
        x,
        middle,
        lines_ref,
        cols_ref,
        couples_ref,
        curve_ref,
        *merged,
        small_sems,
        sems,
    ) = rest[-14:]
    az, odd = position()

    @pl.when((az == 0) if late else (az > 0))
    def _():
        small = start_all(
            (lines_hbm, lines_ref, small_sems.at[0]),
            (cols_hbm, cols_ref, small_sems.at[1]),
            (couples_hbm, couples_ref, small_sems.at[2]),
            (curve_hbm, curve_ref, small_sems.at[3]),
        )
        planes = start_all(
            *(
                (x_hbm.at[p // IMAGES, p % IMAGES, 0], x.at[p], sems.at[p])
                for p in range(PLANES)
            )
        )
        wait_all(small)
        offset = az * BLOCK_HEIGHT - start_ref[0]
        last = BLOCK_HEIGHT - MARGIN

        def take(row, out_ref, wait):
            base = window_base(offset + row)

            def window(p):
                if wait:
                    planes[p].wait()
                return x.at[p, pl.ds(base, WINDOW)]

            take_lines(offset + row, base, window, lines_ref, cols_ref, curve_ref, out_ref)

        take(jnp.where(odd, last, 0), b_out, True)
        take(jnp.where(odd, 0, last), a_out, False)
        take(MARGIN, middle, False)
        sums = box_sums(4, BOXES - 2 * (MARGIN // LOOK_ROWS), (middle,), couples_ref, merged)
        for u in range(3 * PAIRS):
            sums_out[u] = pltpu.roll(sums[u], MARGIN // LOOK_ROWS, 0)


def add_edge(low, sums, sums_ref):
    edge = MARGIN // LOOK_ROWS
    sublane = iota((BOXES, LOOKS), 0)
    first = jnp.where(low, 0, BOXES - edge)
    mine = (sublane >= first) & (sublane < first + edge)
    return [
        jnp.where(
            mine, jnp.where(low, sums[u], pltpu.roll(sums[u], BOXES - edge, 0)), sums_ref[u]
        )
        for u in range(3 * PAIRS)
    ]


def far_kernel(
    couples_vmem, b_ref, own_ref, sums_ref, out_ref, couples_ref, sem, *merged
):
    _, odd = position()
    copies = start_all((couples_vmem, couples_ref, sem))
    sums = box_sums(
        2,
        MARGIN // LOOK_ROWS,
        (b_ref, own_ref),
        couples_ref,
        merged,
        ready=lambda: wait_all(copies),
    )
    for u, value in enumerate(add_edge(jnp.logical_not(odd), sums, sums_ref)):
        out_ref[u] = value


def near_kernel(
    couples_vmem, a_ref, own_ref, sums_ref, ifg_ref, coh_ref, power, couples_ref, sem, *merged
):
    _, odd = position()
    copies = start_all((couples_vmem, couples_ref, sem))
    sums = box_sums(
        2,
        MARGIN // LOOK_ROWS,
        (a_ref, own_ref),
        couples_ref,
        merged,
        ready=lambda: wait_all(copies),
    )
    sums = add_edge(odd, sums, sums_ref)
    for a in range(IMAGES):
        power[a] = sums[2 * PAIRS + a]
    for p in range(PAIRS):
        re, im = sums[p], sums[PAIRS + p]
        ifg_ref[0, p] = re / float(LOOK_ROWS * LOOK_COLS)
        ifg_ref[1, p] = im / float(LOOK_ROWS * LOOK_COLS)
        both = power[couples_ref[p, 0]] * power[couples_ref[p, 1]]
        coh_ref[p] = (re * re + im * im) / jnp.maximum(both, 1.0)


def swaps(n, first):
    pairs = [(k, k + 1) for k in range(first, n - 1, 2)]
    return pairs + [(j, i) for i, j in pairs]


def limit(mebibytes):
    return pltpu.CompilerParams(vmem_limit_bytes=mebibytes * 2**20)


def in_hbm(array):
    return pltpu.with_memory_space_constraint(array, pltpu.HBM)


def per_device(
    sweep_stack,
    blend_curve,
    sweep_start_index,
    usable_azimuth_extent,
    usable_column_extent,
    image_couples,
):
    n = lax.axis_size("az")
    sent = jax.ShapeDtypeStruct((PLANES, SENT, SLANT_WIDTH), BF16)
    sums_shape = jax.ShapeDtypeStruct((3 * PAIRS, BOXES, LOOKS), F32)
    dma = pltpu.SemaphoreType.DMA
    lines_smem = pltpu.SMEM((1, 2), jnp.int32)
    couples_smem = pltpu.SMEM((PAIRS, 2), jnp.int32)
    curve_vmem = pltpu.VMEM((1, SWEEP_HEIGHT), BF16)
    merged = [
        pltpu.VMEM((2, IMAGES, BLOCK_HEIGHT, TILE), F32) for _ in range(SLANT_WIDTH // 2 // TILE)
    ]
    lines, columns, couples, curve, stack = (
        in_hbm(array)
        for array in (
            usable_azimuth_extent,
            usable_column_extent,
            image_couples,
            blend_curve,
            sweep_stack,
        )
    )
    to_a, to_b = pl.pallas_call(
        pack_kernel,
        out_shape=(sent, sent),
        in_specs=[SMEM] + [HBM] * 4,
        out_specs=(VMEM, VMEM),
        scratch_shapes=[
            pltpu.VMEM((2, PLANES, WINDOW, SLANT_WIDTH), BF16),
            lines_smem,
            lines_smem,
            curve_vmem,
            dma((2, PLANES)),
            dma((3,)),
        ],
        compiler_params=limit(16),
        name="pack",
    )(sweep_start_index, lines, columns, curve, stack)
    from_b = lax.ppermute(to_b, "az", swaps(n, 1))
    from_a = lax.ppermute(to_a, "az", swaps(n, 0))

    def own(late, *before):
        return pl.pallas_call(
            functools.partial(own_kernel, late),
            out_shape=(sent, sent, sums_shape),
            in_specs=[SMEM] + [HBM] * 5 + [VMEM] * len(before),
            out_specs=(VMEM, VMEM, VMEM),
            scratch_shapes=[
                pltpu.VMEM((PLANES, SWEEP_HEIGHT, SLANT_WIDTH), BF16),
                pltpu.VMEM((PLANES, SENT, SLANT_WIDTH), BF16),
                lines_smem,
                lines_smem,
                couples_smem,
                curve_vmem,
                *merged[:3],
                dma((4,)),
                dma((PLANES,)),
            ],
            input_output_aliases={6: 0, 7: 1, 8: 2} if before else {},
            compiler_params=limit(24),
            name="late" if late else "early",
        )(sweep_start_index, lines, columns, couples, curve, stack, *before)

    own_a, own_b, sums = own(False)
    own_a, own_b, sums = own(True, own_a, own_b, sums)
    sums = pl.pallas_call(
        far_kernel,
        out_shape=sums_shape,
        in_specs=[VMEM, VMEM, VMEM, VMEM],
        out_specs=VMEM,
        scratch_shapes=[couples_smem, dma, *merged],
        compiler_params=limit(16),
        name="far",
    )(image_couples, from_b, own_b, sums)
    return pl.pallas_call(
        near_kernel,
        out_shape=(
            jax.ShapeDtypeStruct((2, PAIRS, BOXES, LOOKS), F32),
            jax.ShapeDtypeStruct((PAIRS, BOXES, LOOKS), F32),
        ),
        in_specs=[VMEM, VMEM, VMEM, VMEM],
        out_specs=(VMEM, VMEM),
        scratch_shapes=[pltpu.VMEM((IMAGES, BOXES, LOOKS), F32), couples_smem, dma, *merged],
        compiler_params=limit(16),
        name="near",
    )(image_couples, from_a, own_a, sums)


def solution(mesh):
    return jax.shard_map(
        per_device,
        mesh=mesh,
        in_specs=(
            P(None, None, ("groups", "az"), None, None),
            P(("groups", "az"), None),
            P(("groups", "az")),
            P(("groups", "az"), None),
            P(("groups", "az"), None),
            P("groups", None),
        ),
        out_specs=(P(None, "groups", "az", None), P("groups", "az", None)),
        check_vma=False,
    )
```

time: 35.4 us -> 34 us (0.960)
  starting transfers between devices: 20.9 us -> 19.1 us
  local copies, waits for them, and re-layouts: 0.11 us -> 0.67 us
    ppermute x1, starting transfers between devices: 15.8 us -> 14 us  [per_device(): from_a = lax.ppermute(to_a, 'az', swaps(n, 0))]
    pallas_call x3 -> x4, Pallas kernels: 9.49 us -> 7.79 us  [the longest x2 4.26 us: own(): pl.pallas_call(functools.partial(own_kernel, late), out_shape=(sent, sent...]
    pallas_call x1, Pallas kernels: 3.33 us -> 4.88 us  [per_device(): pl.pallas_call(pack_kernel, out_shape=(sent, sent), in_specs=[SMEM] + [HB...]
    unnamed x9 -> x5, local copies, waits for them, and re-layouts: 0.11 us -> 0.67 us
  transfers between devices with their start and end apart: 2 -> 2, of which waited for: 0 -> 0; matrix products, arithmetic and copies ran while one was open for 0% -> 2% of each run, Pallas kernels for 19% -> 17%
where the time goes in v3:
time: 34 us; the launch traced here: 33.8 us
  starting transfers between devices  19.1 us (56%)
  Pallas kernels  12.7 us (37%)
  between operations  1.36 us (4%)
  local copies, waits for them, and re-layouts  0.67 us (2%)
    ppermute x1, starting transfers between devices, per_device(): from_a = lax.ppermute(to_a, 'az', swaps(n, 0))  14 us
    ppermute x1, starting transfers between devices, per_device(): from_b = lax.ppermute(to_b, 'az', swaps(n, 1))  5.09 us
    pallas_call x1, Pallas kernels, per_device(): pl.pallas_call(pack_kernel, out_shape=(sent, sent), in_specs=[SMEM] + [HB...  4.88 us
    pallas_call x2, Pallas kernels, own(): pl.pallas_call(functools.partial(own_kernel, late), out_shape=(sent, sent...  4.26 us
    pallas_call x1, Pallas kernels, per_device(): pl.pallas_call(near_kernel, out_shape=(jax.ShapeDtypeStruct((2, PAIRS, BO...  2.13 us
    pallas_call x1, Pallas kernels, per_device(): pl.pallas_call(far_kernel, out_shape=sums_shape, in_specs=[VMEM, VMEM, VM...  1.41 us
  transfers between devices with their start and end apart: 2, of which 0 were waited for; matrix products, arithmetic and copies ran while one was open for 2% of the time, Pallas kernels for 17%

profile of v3, /device:TPU:37, one launch (start us, length us, event | category | flops | bytes accessed | tf_op | source)
XLA Modules:
  0.0 33.8 jit_solution(8020796634244294533)
XLA Ops:
  0.6 0.0 copy-start.1
  1.3 4.9 %pack.1 = (bf16[8,16,2560]{2,1,0:T(8,128)(2,1)S(1)}, bf16[8,16,2560]{2,1,0:T(8,128)(2,1)S(1)}) custom-call(s32[1]{0:T(128)S(6)} %copy.18.start_ref, s32[1,2]{1,0:T(1,128)} %lines_hbm.5, s32[1,2]{1,0:T(1,128)} %cols_hbm.5, bf16[1,80]{1,0:T(2,128)(2,1)} %curve_hbm.5, bf16[2,4,1,80,2560]{4,3,2,1,0:T(8,128)(2,1)} %x_hbm.5), custom_call_target="tpu_custom_call" | custom-call | tf_op jit(solution)/shard_map/pack/pallas_call | solution.py:383
  6.2 5.1 %collective-permute-start.1 = (bf16[8,16,2560]{2,1,0:T(8,128)(2,1)S(1)}, bf16[8,16,2560]{2,1,0:T(8,128)(2,1)S(1)}, u32[]{:S(2)}, u32[]{:S(2)}) collective-permute-start(bf16[8,16,2560]{2,1,0:T(8,128)(2,1)S(1)} %get-tuple-element.15), channel_id=1, source_target_pairs={{1,2},{3,4},{5,6},{7,8},{9,10},{11,12},{13,14},{15,16},{17,18},{19... | collective-permute-start | bytes 1966088 | tf_op jit(solution)/shard_map/ppermute | solution.py:399
  11.3 14.0 %collective-permute-start = (bf16[8,16,2560]{2,1,0:T(8,128)(2,1)S(1)}, bf16[8,16,2560]{2,1,0:T(8,128)(2,1)S(1)}, u32[]{:S(2)}, u32[]{:S(2)}) collective-permute-start(bf16[8,16,2560]{2,1,0:T(8,128)(2,1)S(1)} %get-tuple-element.10), channel_id=1, source_target_pairs={{0,1},{2,3},{4,5},{6,7},{8,9},{10,11},{12,13},{14,15},{16,17},{18,... | collective-permute-start | bytes 1966088 | tf_op jit(solution)/shard_map/ppermute | solution.py:400
  25.3 0.0 copy-done.1
  25.3 0.7 %copy.14.couples_hbm.couples_vmem = s32[4,2]{1,0:T(4,128)} copy(s32[4,2]{0,1:T(2,128)S(1)} %copy-done.1) | data formatting | bytes 64 | tf_op args[5]
  26.0 0.0 copy-start
  26.0 4.1 %early.1 = (bf16[8,16,2560]{2,1,0:T(8,128)(2,1)S(1)}, bf16[8,16,2560]{2,1,0:T(8,128)(2,1)S(1)}, f32[12,8,128]{2,1,0:T(8,128)S(1)}) custom-call(s32[1]{0:T(128)S(6)} %copy.18.start_ref, s32[1,2]{1,0:T(1,128)} %lines_hbm.5, s32[1,2]{1,0:T(1,128)} %cols_hbm.5, s32[4,2]{1,0:T(4,128)} %copy.14.couples_hbm.couples_vmem, bf16[1,80]{1,0:T(2,128)(2,1)} %curve_hbm.5, ...), custom_call_target="tpu_custom_call" | custom-call | tf_op jit(solution)/shard_map/early/pallas_call | solution.py:403
  30.1 0.1 late.1
  30.2 0.0 collective-permute-done.1.b_ref
  30.2 0.0 copy-done
  30.2 1.4 %far.1.sums_ref = f32[12,8,128]{2,1,0:T(8,128)S(1)} custom-call(s32[4,2]{1,0:T(4,128)S(1)} %copy-done, bf16[8,16,2560]{2,1,0:T(8,128)(2,1)S(1)} %collective-permute-done.1.b_ref, bf16[8,16,2560]{2,1,0:T(8,128)(2,1)S(1)} %get-tuple-element.16.own_ref, f32[12,8,128]{2,1,0:T(8,128)S(1)} %get-tuple-element.17.sums_ref), custom_call_target="tpu_custom_call" | custom-call | tf_op jit(solution)/shard_map/far/pallas_call | solution.py:426
  31.7 0.0 collective-permute-done.a_ref
  31.7 2.1 %near.1 = (f32[2,4,8,128]{3,2,1,0:T(8,128)}, f32[4,8,128]{2,1,0:T(8,128)}) custom-call(s32[4,2]{1,0:T(4,128)S(1)} %copy-done, bf16[8,16,2560]{2,1,0:T(8,128)(2,1)S(1)} %collective-permute-done.a_ref, bf16[8,16,2560]{2,1,0:T(8,128)(2,1)S(1)} %get-tuple-element.14.own_ref, f32[12,8,128]{2,1,0:T(8,128)S(1)} %far.1.sums_ref), custom_call_target="tpu_custom_call" | custom-call | tf_op jit(solution)/shard_map/near/pallas_call | solution.py:435
Async XLA Ops:
  0.6 24.7 %copy-start.1 = (s32[4,2]{0,1:T(2,128)S(1)}, s32[4,2]{0,1:T(2,128)}, u32[]{:S(2)}) copy-start(s32[4,2]{0,1:T(2,128)} %param.11) | copy-start | bytes 100
  6.2 24.0 %collective-permute-start.1 = (bf16[8,16,2560]{2,1,0:T(8,128)(2,1)S(1)}, bf16[8,16,2560]{2,1,0:T(8,128)(2,1)S(1)}, u32[]{:S(2)}, u32[]{:S(2)}) collective-permute-start(bf16[8,16,2560]{2,1,0:T(8,128)(2,1)S(1)} %get-tuple-element.15), channel_id=1, source_target_pairs={{1,2},{3,4},{5,6},{7,8},{9,10},{11,12},{13,14},{15,16},{17,18},{19... | collective-permute-start | bytes 1966088 | tf_op jit(solution)/shard_map/ppermute | solution.py:399
  11.3 20.4 %collective-permute-start = (bf16[8,16,2560]{2,1,0:T(8,128)(2,1)S(1)}, bf16[8,16,2560]{2,1,0:T(8,128)(2,1)S(1)}, u32[]{:S(2)}, u32[]{:S(2)}) collective-permute-start(bf16[8,16,2560]{2,1,0:T(8,128)(2,1)S(1)} %get-tuple-element.10), channel_id=1, source_target_pairs={{0,1},{2,3},{4,5},{6,7},{8,9},{10,11},{12,13},{14,15},{16,17},{18,... | collective-permute-start | bytes 1966088 | tf_op jit(solution)/shard_map/ppermute | solution.py:400
  26.0 4.3 %copy-start = (s32[4,2]{1,0:T(4,128)S(1)}, s32[4,2]{1,0:T(4,128)}, u32[]{:S(2)}) copy-start(s32[4,2]{1,0:T(4,128)} %copy.14.couples_hbm.couples_vmem) | copy-start | bytes 100

commit v4 on v3

--- a/solution.py
+++ b/solution.py
@@ -134,11 +134,16 @@
     wait_all(small)
 
     def take(side, copies, out_ref):
-        def window(p):
-            copies[p].wait()
-            return windows.at[side, p]
-
-        take_lines(firsts[side], bases[side], window, lines_ref, cols_ref, curve_ref, out_ref)
+        wait_all(copies)
+        take_lines(
+            firsts[side],
+            bases[side],
+            lambda p: windows.at[side, p],
+            lines_ref,
+            cols_ref,
+            curve_ref,
+            out_ref,
+        )
 
     take(0, near, a_ref)
 
@@ -151,7 +156,7 @@
     return ref[0, MARGIN:SENT, :SENT].astype(F32)
 
 
-def box_sums(parts, boxes, sources, couples_ref, merged_refs, ready=None):
+def box_sums(parts, boxes, sources, cells_ref, couples_ref, merged_refs, ready=None):
     stride = BOXES // parts
     width = SLANT_WIDTH // parts
     slot = iota((BLOCK_HEIGHT, SENT), 0)
@@ -167,7 +172,9 @@
         [jnp.where(part == q, w, 0.0) for q in range(parts) for w in chosen], axis=1
     ).astype(BF16)
     tiles = [(at, min(TILE, width - at)) for at in range(0, width, TILE)]
-    for (at, size), merged in zip(tiles, merged_refs):
+
+    def merge(t):
+        (at, size), merged = tiles[t], merged_refs[t]
         for p in range(PLANES):
             values = jnp.concatenate(
                 [
@@ -180,11 +187,9 @@
             merged[p // IMAGES, p % IMAGES, :, :size] = (
                 jnp.dot(select, values, preferred_element_type=F32) * scale[:, :size]
             )
-    if ready is not None:
-        ready()
-    couples = [(couples_ref[p, 0], couples_ref[p, 1]) for p in range(PAIRS)]
-    acc = None
-    for (at, size), merged in zip(tiles, merged_refs):
+
+    def look(t, couples):
+        (at, size), merged = tiles[t], merged_refs[t]
 
         def rows(v):
             return jnp.sum(v.reshape(LOOK_ROWS, BOXES, size), axis=0)
@@ -203,12 +208,21 @@
         sums = jnp.concatenate(real + imag + powers, axis=0)
         high = sums.astype(BF16)
         low = (sums - high.astype(F32)).astype(BF16)
-        where = iota((size, LOOKS), 0) + at
-        look = iota((size, LOOKS), 1) * LOOK_COLS
-        cells = as_bf16((where >= look) & (where < look + LOOK_COLS))
-        got = jnp.dot(high, cells, preferred_element_type=F32) + jnp.dot(
+        cells = cells_ref[at : at + size, :]
+        return jnp.dot(high, cells, preferred_element_type=F32) + jnp.dot(
             low, cells, preferred_element_type=F32
         )
+
+    merge(0)
+    merge(1)
+    if ready is not None:
+        ready()
+    couples = [(couples_ref[0, p], couples_ref[1, p]) for p in range(PAIRS)]
+    acc = None
+    for t in range(len(tiles)):
+        if t + 2 < len(tiles):
+            merge(t + 2)
+        got = look(t, couples)
         acc = got if acc is None else acc + got
     lane = iota((BOXES, LOOKS), 1)
     step = LOOKS // parts
@@ -237,6 +251,7 @@
         a_out,
         b_out,
         sums_out,
+        cells_out,
         x,
         middle,
         lines_ref,
@@ -246,7 +261,7 @@
         *merged,
         small_sems,
         sems,
-    ) = rest[-14:]
+    ) = rest[-15:]
     az, odd = position()
 
     @pl.when((az == 0) if late else (az > 0))
@@ -263,24 +278,32 @@
                 for p in range(PLANES)
             )
         )
-        wait_all(small)
+        wait_all(small + planes)
         offset = az * BLOCK_HEIGHT - start_ref[0]
         last = BLOCK_HEIGHT - MARGIN
 
-        def take(row, out_ref, wait):
+        def take(row, out_ref):
             base = window_base(offset + row)
 
-            def window(p):
-                if wait:
-                    planes[p].wait()
-                return x.at[p, pl.ds(base, WINDOW)]
-
-            take_lines(offset + row, base, window, lines_ref, cols_ref, curve_ref, out_ref)
-
-        take(jnp.where(odd, last, 0), b_out, True)
-        take(jnp.where(odd, 0, last), a_out, False)
-        take(MARGIN, middle, False)
-        sums = box_sums(4, BOXES - 2 * (MARGIN // LOOK_ROWS), (middle,), couples_ref, merged)
+            take_lines(
+                offset + row,
+                base,
+                lambda p: x.at[p, pl.ds(base, WINDOW)],
+                lines_ref,
+                cols_ref,
+                curve_ref,
+                out_ref,
+            )
+
+        take(jnp.where(odd, last, 0), b_out)
+        take(jnp.where(odd, 0, last), a_out)
+        take(MARGIN, middle)
+        for at in range(0, SLANT_WIDTH // 2, TILE):
+            where = iota((TILE, LOOKS), 0) + at
+            look = iota((TILE, LOOKS), 1) * LOOK_COLS
+            cells_out[at : at + TILE, :] = as_bf16((where >= look) & (where < look + LOOK_COLS))
+        boxes = BOXES - 2 * (MARGIN // LOOK_ROWS)
+        sums = box_sums(4, boxes, (middle,), cells_out, couples_ref, merged)
         for u in range(3 * PAIRS):
             sums_out[u] = pltpu.roll(sums[u], MARGIN // LOOK_ROWS, 0)
 
@@ -299,7 +322,7 @@
 
 
 def far_kernel(
-    couples_vmem, b_ref, own_ref, sums_ref, out_ref, couples_ref, sem, *merged
+    couples_vmem, b_ref, own_ref, sums_ref, cells_ref, out_ref, couples_ref, sem, *merged
 ):
     _, odd = position()
     copies = start_all((couples_vmem, couples_ref, sem))
@@ -307,6 +330,7 @@
         2,
         MARGIN // LOOK_ROWS,
         (b_ref, own_ref),
+        cells_ref,
         couples_ref,
         merged,
         ready=lambda: wait_all(copies),
@@ -316,7 +340,17 @@
 
 
 def near_kernel(
-    couples_vmem, a_ref, own_ref, sums_ref, ifg_ref, coh_ref, power, couples_ref, sem, *merged
+    couples_vmem,
+    a_ref,
+    own_ref,
+    sums_ref,
+    cells_ref,
+    ifg_ref,
+    coh_ref,
+    power,
+    couples_ref,
+    sem,
+    *merged,
 ):
     _, odd = position()
     copies = start_all((couples_vmem, couples_ref, sem))
@@ -324,6 +358,7 @@
         2,
         MARGIN // LOOK_ROWS,
         (a_ref, own_ref),
+        cells_ref,
         couples_ref,
         merged,
         ready=lambda: wait_all(copies),
@@ -335,7 +370,7 @@
         re, im = sums[p], sums[PAIRS + p]
         ifg_ref[0, p] = re / float(LOOK_ROWS * LOOK_COLS)
         ifg_ref[1, p] = im / float(LOOK_ROWS * LOOK_COLS)
-        both = power[couples_ref[p, 0]] * power[couples_ref[p, 1]]
+        both = power[couples_ref[0, p]] * power[couples_ref[1, p]]
         coh_ref[p] = (re * re + im * im) / jnp.maximum(both, 1.0)
 
 
@@ -363,19 +398,21 @@
     n = lax.axis_size("az")
     sent = jax.ShapeDtypeStruct((PLANES, SENT, SLANT_WIDTH), BF16)
     sums_shape = jax.ShapeDtypeStruct((3 * PAIRS, BOXES, LOOKS), F32)
+    cells_shape = jax.ShapeDtypeStruct((SLANT_WIDTH // 2, LOOKS), BF16)
     dma = pltpu.SemaphoreType.DMA
     lines_smem = pltpu.SMEM((1, 2), jnp.int32)
-    couples_smem = pltpu.SMEM((PAIRS, 2), jnp.int32)
+    couples_smem = pltpu.SMEM((2, PAIRS), jnp.int32)
     curve_vmem = pltpu.VMEM((1, SWEEP_HEIGHT), BF16)
     merged = [
         pltpu.VMEM((2, IMAGES, BLOCK_HEIGHT, TILE), F32) for _ in range(SLANT_WIDTH // 2 // TILE)
     ]
-    lines, columns, couples, curve, stack = (
+    couples = image_couples.T
+    lines, columns, couples_hbm, curve, stack = (
         in_hbm(array)
         for array in (
             usable_azimuth_extent,
             usable_column_extent,
-            image_couples,
+            couples,
             blend_curve,
             sweep_stack,
         )
@@ -402,9 +439,9 @@
     def own(late, *before):
         return pl.pallas_call(
             functools.partial(own_kernel, late),
-            out_shape=(sent, sent, sums_shape),
+            out_shape=(sent, sent, sums_shape, cells_shape),
             in_specs=[SMEM] + [HBM] * 5 + [VMEM] * len(before),
-            out_specs=(VMEM, VMEM, VMEM),
+            out_specs=(VMEM,) * 4,
             scratch_shapes=[
                 pltpu.VMEM((PLANES, SWEEP_HEIGHT, SLANT_WIDTH), BF16),
                 pltpu.VMEM((PLANES, SENT, SLANT_WIDTH), BF16),
@@ -416,34 +453,34 @@
                 dma((4,)),
                 dma((PLANES,)),
             ],
-            input_output_aliases={6: 0, 7: 1, 8: 2} if before else {},
+            input_output_aliases={6 + k: k for k in range(len(before))},
             compiler_params=limit(24),
             name="late" if late else "early",
-        )(sweep_start_index, lines, columns, couples, curve, stack, *before)
-
-    own_a, own_b, sums = own(False)
-    own_a, own_b, sums = own(True, own_a, own_b, sums)
+        )(sweep_start_index, lines, columns, couples_hbm, curve, stack, *before)
+
+    mine = own(False)
+    own_a, own_b, sums, cells = own(True, *mine)
     sums = pl.pallas_call(
         far_kernel,
         out_shape=sums_shape,
-        in_specs=[VMEM, VMEM, VMEM, VMEM],
+        in_specs=[VMEM] * 5,
         out_specs=VMEM,
         scratch_shapes=[couples_smem, dma, *merged],
         compiler_params=limit(16),
         name="far",
-    )(image_couples, from_b, own_b, sums)
+    )(couples, from_b, own_b, sums, cells)
     return pl.pallas_call(
         near_kernel,
         out_shape=(
             jax.ShapeDtypeStruct((2, PAIRS, BOXES, LOOKS), F32),
             jax.ShapeDtypeStruct((PAIRS, BOXES, LOOKS), F32),
         ),
-        in_specs=[VMEM, VMEM, VMEM, VMEM],
+        in_specs=[VMEM] * 5,
         out_specs=(VMEM, VMEM),
         scratch_shapes=[pltpu.VMEM((IMAGES, BOXES, LOOKS), F32), couples_smem, dma, *merged],
         compiler_params=limit(16),
         name="near",
-    )(image_couples, from_a, own_a, sums)
+    )(couples, from_a, own_a, sums, cells)
 
 
 def solution(mesh):

time: 34 us -> 32.4 us (0.953)
  Pallas kernels: 12.7 us -> 10.8 us
  starting transfers between devices: 19.1 us -> 19.6 us
    pallas_call x1, Pallas kernels: 4.88 us -> 3.54 us  [per_device(): pl.pallas_call(pack_kernel, out_shape=(sent, sent), in_specs=[SMEM] + [HB...]
    pallas_call x2, Pallas kernels: 4.26 us -> 3.57 us  [own(): pl.pallas_call(functools.partial(own_kernel, late), out_shape=(sent, sent...]
    ppermute x1, starting transfers between devices: 14 us -> 14.5 us  [per_device(): from_a = lax.ppermute(to_a, 'az', swaps(n, 0))]
  transfers between devices with their start and end apart: 2 -> 2, of which waited for: 0 -> 0; matrix products, arithmetic and copies ran while one was open for 2% -> 0% of each run, Pallas kernels for 17% -> 16%
where the time goes in v4:
time: 32.4 us; the launch traced here: 32.2 us
  starting transfers between devices  19.6 us (60%)
  Pallas kernels  10.8 us (33%)
  between operations  1.34 us (4%)
  local copies, waits for them, and re-layouts  0.53 us (2%)
    ppermute x1, starting transfers between devices, per_device(): from_a = lax.ppermute(to_a, 'az', swaps(n, 0))  14.5 us
    ppermute x1, starting transfers between devices, per_device(): from_b = lax.ppermute(to_b, 'az', swaps(n, 1))  5.08 us
    pallas_call x2, Pallas kernels, own(): pl.pallas_call(functools.partial(own_kernel, late), out_shape=(sent, sent...  3.57 us
    pallas_call x1, Pallas kernels, per_device(): pl.pallas_call(pack_kernel, out_shape=(sent, sent), in_specs=[SMEM] + [HB...  3.54 us
    pallas_call x1, Pallas kernels, per_device(): pl.pallas_call(near_kernel, out_shape=(jax.ShapeDtypeStruct((2, PAIRS, BO...  2.15 us
    pallas_call x1, Pallas kernels, per_device(): pl.pallas_call(far_kernel, out_shape=sums_shape, in_specs=[VMEM] * 5, out...  1.51 us
  transfers between devices with their start and end apart: 2, of which 0 were waited for; matrix products, arithmetic and copies ran while one was open for 0% of the time, Pallas kernels for 16%

profile of v4, /device:TPU:37, one launch (start us, length us, event | category | flops | bytes accessed | tf_op | source)
XLA Modules:
  0.0 32.2 jit_solution(10115508143889247862)
XLA Ops:
  1.3 3.5 %pack.1 = (bf16[8,16,2560]{2,1,0:T(8,128)(2,1)S(1)}, bf16[8,16,2560]{2,1,0:T(8,128)(2,1)S(1)}) custom-call(s32[1]{0:T(128)S(6)} %copy.16.start_ref, s32[1,2]{1,0:T(1,128)} %lines_hbm.5, s32[1,2]{1,0:T(1,128)} %cols_hbm.5, bf16[1,80]{1,0:T(2,128)(2,1)} %curve_hbm.5, bf16[2,4,1,80,2560]{4,3,2,1,0:T(8,128)(2,1)} %x_hbm.5), custom_call_target="tpu_custom_call" | custom-call | tf_op jit(solution)/shard_map/pack/pallas_call | solution.py:420
  4.8 5.1 %collective-permute-start.1 = (bf16[8,16,2560]{2,1,0:T(8,128)(2,1)S(1)}, bf16[8,16,2560]{2,1,0:T(8,128)(2,1)S(1)}, u32[]{:S(2)}, u32[]{:S(2)}) collective-permute-start(bf16[8,16,2560]{2,1,0:T(8,128)(2,1)S(1)} %get-tuple-element.18), channel_id=1, source_target_pairs={{1,2},{3,4},{5,6},{7,8},{9,10},{11,12},{13,14},{15,16},{17,18},{19... | collective-permute-start | bytes 1966088 | tf_op jit(solution)/shard_map/ppermute | solution.py:436
  9.9 14.5 %collective-permute-start = (bf16[8,16,2560]{2,1,0:T(8,128)(2,1)S(1)}, bf16[8,16,2560]{2,1,0:T(8,128)(2,1)S(1)}, u32[]{:S(2)}, u32[]{:S(2)}) collective-permute-start(bf16[8,16,2560]{2,1,0:T(8,128)(2,1)S(1)} %get-tuple-element.12), channel_id=1, source_target_pairs={{0,1},{2,3},{4,5},{6,7},{8,9},{10,11},{12,13},{14,15},{16,17},{18,... | collective-permute-start | bytes 1966088 | tf_op jit(solution)/shard_map/ppermute | solution.py:437
  24.4 3.4 %early.1 = (bf16[8,16,2560]{2,1,0:T(8,128)(2,1)S(1)}, bf16[8,16,2560]{2,1,0:T(8,128)(2,1)S(1)}, f32[12,8,128]{2,1,0:T(8,128)S(1)}, bf16[1280,128]{1,0:T(8,128)(2,1)S(1)}) custom-call(s32[1]{0:T(128)S(6)} %copy.16.start_ref, s32[1,2]{1,0:T(1,128)} %lines_hbm.5, s32[1,2]{1,0:T(1,128)} %cols_hbm.5, s32[2,4]{1,0:T(2,128)} %bitcast.1, bf16[1,80]{1,0:T(2,128)(2,1)} %curve_hbm.5, ...), custom_call_target="tpu_custom_call" | custom-call | tf_op jit(solution)/shard_map/early/pallas_call | solution.py:440
  27.9 0.0 copy-start
  27.9 0.1 late.1
  28.0 0.0 collective-permute-done.1.b_ref
  28.0 0.5 %copy-done = s32[4,2]{0,1:T(2,128)S(1)} copy-done((s32[4,2]{0,1:T(2,128)S(1)}, s32[4,2]{0,1:T(2,128)}, u32[]{:S(2)}) %copy-start) | copy-done | bytes 56
  28.6 1.5 %far.1.sums_ref = f32[12,8,128]{2,1,0:T(8,128)S(1)} custom-call(s32[2,4]{1,0:T(2,128)S(1)} %bitcast.3, bf16[8,16,2560]{2,1,0:T(8,128)(2,1)S(1)} %collective-permute-done.1.b_ref, bf16[8,16,2560]{2,1,0:T(8,128)(2,1)S(1)} %get-tuple-element.19.own_ref, f32[12,8,128]{2,1,0:T(8,128)S(1)} %get-tuple-element.20.sums_ref, ...), custom_call_target="tpu_custom_call" | custom-call | tf_op jit(solution)/shard_map/far/pallas_call | solution.py:463
  30.1 0.0 collective-permute-done.a_ref
  30.1 2.1 %near.1 = (f32[2,4,8,128]{3,2,1,0:T(8,128)}, f32[4,8,128]{2,1,0:T(8,128)}) custom-call(s32[2,4]{1,0:T(2,128)S(1)} %bitcast.4, bf16[8,16,2560]{2,1,0:T(8,128)(2,1)S(1)} %collective-permute-done.a_ref, bf16[8,16,2560]{2,1,0:T(8,128)(2,1)S(1)} %get-tuple-element.17.own_ref, f32[12,8,128]{2,1,0:T(8,128)S(1)} %far.1.sums_ref, ...), custom_call_target="tpu_custom_call" | custom-call | tf_op jit(solution)/shard_map/near/pallas_call | solution.py:472
Async XLA Ops:
  4.8 23.2 %collective-permute-start.1 = (bf16[8,16,2560]{2,1,0:T(8,128)(2,1)S(1)}, bf16[8,16,2560]{2,1,0:T(8,128)(2,1)S(1)}, u32[]{:S(2)}, u32[]{:S(2)}) collective-permute-start(bf16[8,16,2560]{2,1,0:T(8,128)(2,1)S(1)} %get-tuple-element.18), channel_id=1, source_target_pairs={{1,2},{3,4},{5,6},{7,8},{9,10},{11,12},{13,14},{15,16},{17,18},{19... | collective-permute-start | bytes 1966088 | tf_op jit(solution)/shard_map/ppermute | solution.py:436
  9.9 20.2 %collective-permute-start = (bf16[8,16,2560]{2,1,0:T(8,128)(2,1)S(1)}, bf16[8,16,2560]{2,1,0:T(8,128)(2,1)S(1)}, u32[]{:S(2)}, u32[]{:S(2)}) collective-permute-start(bf16[8,16,2560]{2,1,0:T(8,128)(2,1)S(1)} %get-tuple-element.12), channel_id=1, source_target_pairs={{0,1},{2,3},{4,5},{6,7},{8,9},{10,11},{12,13},{14,15},{16,17},{18,... | collective-permute-start | bytes 1966088 | tf_op jit(solution)/shard_map/ppermute | solution.py:437
  27.9 0.7 %copy-start = (s32[4,2]{0,1:T(2,128)S(1)}, s32[4,2]{0,1:T(2,128)}, u32[]{:S(2)}) copy-start(s32[4,2]{0,1:T(2,128)} %param.11) | copy-start | bytes 100
